TPU v7x, 8 devices: a whole 2x2x1 slice. The times are simulated.
8 devices in a mesh: stage: 1 (over z), fsdp: 2 (over y), tp: 4 (over x, core).
Axes of the slice: x: 2, y: 2, z: 1, core: 2. Of those that a mesh axis runs over, the one named last changes fastest.
Arguments:
- weight: float32 [2, 8192, 3072], P('stage', 'fsdp', 'tp')
- momentum: float32 [2, 8192, 3072], P('stage', 'fsdp', 'tp')
- gradient: bfloat16 [2, 8192, 3072], P('stage', 'fsdp', 'tp')
- learn_rate: float32 [], replicated
- mom_coef: float32 [], replicated
- weight_decay: float32 [], replicated
Outputs:
- output 1: float32 [2, 8192, 3072], P('stage', 'fsdp', 'tp')
- output 2: float32 [2, 8192, 3072], P('stage', 'fsdp', 'tp')
All inputs are finite; a program needn't handle non-finite values.
Results may differ from a plain program's by a relative error of at most 0.0108.
Values are sent between devices in bfloat16 or wider.
A program may use at most 1 GiB of HBM per device.

v0:
```python
import jax
import jax.numpy as jnp
from jax import lax
from jax.sharding import PartitionSpec as P
import math

NS_STEPS = 5
COEF_A = 3.4445
COEF_B = -4.7750
COEF_C = 2.0315
NORM_EPS = 1e-7


def solution(mesh):
    fsdp_size = mesh.shape['fsdp']
    mat_spec = P('stage', 'fsdp', 'tp')
    scalar_spec = P()

    def local_step(weight, momentum, gradient, learn_rate, mom_coef, weight_decay):
        row_dim = weight.shape[1] * fsdp_size
        grad_full = gradient.astype(jnp.float32)
        mom_new = mom_coef * momentum + grad_full
        nesterov = grad_full + mom_coef * mom_new
        sq_sum = lax.psum(jnp.sum(nesterov * nesterov, axis=(1, 2)), ('fsdp', 'tp'))
        norm_val = jnp.sqrt(sq_sum)[:, None, None]
        x_iter = (nesterov / (norm_val + NORM_EPS)).astype(jnp.bfloat16)
        for step_idx in range(NS_STEPS):
            x_rows = lax.all_gather(x_iter, 'tp', axis=2, tiled=True)
            gram_part = jnp.einsum('erc,erd->ecd', x_iter, x_rows, preferred_element_type=jnp.float32)
            gram_blk = lax.psum_scatter(gram_part, 'fsdp', scatter_dimension=2, tiled=True).astype(jnp.bfloat16)
            gram_cols = lax.all_gather(gram_blk, 'tp', axis=1, tiled=True)
            gram_rows = lax.all_gather(gram_blk, 'fsdp', axis=2, tiled=True)
            gram_sq = jnp.einsum('eab,ebc->eac', gram_rows, gram_cols, preferred_element_type=jnp.float32).astype(jnp.bfloat16)
            poly_blk = (COEF_B * gram_blk.astype(jnp.float32) + COEF_C * gram_sq.astype(jnp.float32)).astype(jnp.bfloat16)
            poly_rows = lax.all_gather(poly_blk, 'fsdp', axis=2, tiled=True)
            update = jnp.einsum('erk,eck->erc', x_rows, poly_rows, preferred_element_type=jnp.float32)
            x_iter = (COEF_A * x_iter.astype(jnp.float32) + update).astype(jnp.bfloat16)
        step_scale = learn_rate * 0.2 * math.sqrt(row_dim)
        new_weight = (1.0 - learn_rate * weight_decay) * weight - step_scale * x_iter.astype(jnp.float32)
        return new_weight, mom_new

    return jax.shard_map(local_step, mesh=mesh, in_specs=(mat_spec,) * 3 + (scalar_spec,) * 3, out_specs=(mat_spec, mat_spec), check_vma=False)
```

profile of v0, /device:TPU:0, one launch (start us, length us, event | category | flops | bytes accessed | tf_op | source)
XLA Modules:
  0.0 4994.8 jit_solution(2431223205458306801)
XLA Ops:
  7.9 21.5 multiply_reduce_fusion
  29.4 25.0 psum.7
  54.4 17.6 divide_convert_fusion
  72.6 297.2 %all-gather.21.cloned.1.call-done = bf16[2,4096,3072]{2,1,0:T(8,128)(2,1)} async-done(((bf16[2,4096,768]{2,1,0:T(8,128)(2,1)}), bf16[2,4096,3072]{2,1,0:T(8,128)(2,1)}) %all-gather.21.cloned.1.call-update) | async-done | bytes 50331664 | tf_op jit(solution)/shard_map/all_gather | solution.py:28
  369.8 48.7 fusion
  418.6 209.0 %reduce-scatter.6.cloned.1.call-done = f32[2,768,1536]{2,1,0:T(8,128)} async-done(((f32[2,768,3072]{2,1,0:T(8,128)}), f32[2,768,1536]{2,1,0:T(8,128)}) %reduce-scatter.6.cloned.1.call-update) | async-done | bytes 9437200 | tf_op jit(solution)/shard_map/reduce_scatter | solution.py:30
  627.5 6.4 convert_element_type.117
  634.8 115.4 %all-gather.23.cloned.1.call-done = bf16[2,768,3072]{2,1,0:T(8,128)(2,1)} async-done(((bf16[2,768,1536]{2,1,0:T(8,128)(2,1)}), bf16[2,768,3072]{2,1,0:T(8,128)(2,1)}) %all-gather.23.cloned.1.call-update) | async-done | bytes 9437200 | tf_op jit(solution)/shard_map/all_gather | solution.py:32
  750.2 117.5 %all-gather.25.cloned.1.call-done = bf16[2,3072,1536]{2,1,0:T(8,128)(2,1)} async-done(((bf16[2,768,1536]{2,1,0:T(8,128)(2,1)}), bf16[2,3072,1536]{2,1,0:T(8,128)(2,1)}) %all-gather.25.cloned.1.call-update) | async-done | bytes 18874384 | tf_op jit(solution)/shard_map/all_gather | solution.py:31
  867.7 22.5 add_convert_fusion.9
  890.3 116.1 %all-gather.27.cloned.1.call-done = bf16[2,768,3072]{2,1,0:T(8,128)(2,1)} async-done(((bf16[2,768,1536]{2,1,0:T(8,128)(2,1)}), bf16[2,768,3072]{2,1,0:T(8,128)(2,1)}) %all-gather.27.cloned.1.call-update) | async-done | bytes 9437200 | tf_op jit(solution)/shard_map/all_gather | solution.py:35
  1006.4 48.6 add_convert_fusion.4
  1055.3 296.6 %all-gather.29.cloned.1.call-done = bf16[2,4096,3072]{2,1,0:T(8,128)(2,1)} async-done(((bf16[2,4096,768]{2,1,0:T(8,128)(2,1)}), bf16[2,4096,3072]{2,1,0:T(8,128)(2,1)}) %all-gather.29.cloned.1.call-update) | async-done | bytes 50331664 | tf_op jit(solution)/shard_map/all_gather | solution.py:28
  1352.0 48.7 fusion.1
  1400.8 209.0 %reduce-scatter.8.cloned.1.call-done = f32[2,768,1536]{2,1,0:T(8,128)} async-done(((f32[2,768,3072]{2,1,0:T(8,128)}), f32[2,768,1536]{2,1,0:T(8,128)}) %reduce-scatter.8.cloned.1.call-update) | async-done | bytes 9437200 | tf_op jit(solution)/shard_map/reduce_scatter | solution.py:30
  1609.7 6.4 convert_element_type.124
  1617.4 115.0 %all-gather.31.cloned.1.call-done = bf16[2,768,3072]{2,1,0:T(8,128)(2,1)} async-done(((bf16[2,768,1536]{2,1,0:T(8,128)(2,1)}), bf16[2,768,3072]{2,1,0:T(8,128)(2,1)}) %all-gather.31.cloned.1.call-update) | async-done | bytes 9437200 | tf_op jit(solution)/shard_map/all_gather | solution.py:32
  1732.4 117.6 %all-gather.33.cloned.1.call-done = bf16[2,3072,1536]{2,1,0:T(8,128)(2,1)} async-done(((bf16[2,768,1536]{2,1,0:T(8,128)(2,1)}), bf16[2,3072,1536]{2,1,0:T(8,128)(2,1)}) %all-gather.33.cloned.1.call-update) | async-done | bytes 18874384 | tf_op jit(solution)/shard_map/all_gather | solution.py:31
  1850.0 22.5 add_convert_fusion.8
  1872.6 116.1 %all-gather.35.cloned.1.call-done = bf16[2,768,3072]{2,1,0:T(8,128)(2,1)} async-done(((bf16[2,768,1536]{2,1,0:T(8,128)(2,1)}), bf16[2,768,3072]{2,1,0:T(8,128)(2,1)}) %all-gather.35.cloned.1.call-update) | async-done | bytes 9437200 | tf_op jit(solution)/shard_map/all_gather | solution.py:35
  1988.8 48.6 add_convert_fusion.3
  2037.6 296.7 %all-gather.37.cloned.1.call-done = bf16[2,4096,3072]{2,1,0:T(8,128)(2,1)} async-done(((bf16[2,4096,768]{2,1,0:T(8,128)(2,1)}), bf16[2,4096,3072]{2,1,0:T(8,128)(2,1)}) %all-gather.37.cloned.1.call-update) | async-done | bytes 50331664 | tf_op jit(solution)/shard_map/all_gather | solution.py:28
  2334.3 48.7 fusion.2
  2383.1 209.0 %reduce-scatter.10.cloned.1.call-done = f32[2,768,1536]{2,1,0:T(8,128)} async-done(((f32[2,768,3072]{2,1,0:T(8,128)}), f32[2,768,1536]{2,1,0:T(8,128)}) %reduce-scatter.10.cloned.1.call-update) | async-done | bytes 9437200 | tf_op jit(solution)/shard_map/reduce_scatter | solution.py:30
  2592.1 6.4 convert_element_type.131
  2599.4 115.3 %all-gather.39.cloned.1.call-done = bf16[2,768,3072]{2,1,0:T(8,128)(2,1)} async-done(((bf16[2,768,1536]{2,1,0:T(8,128)(2,1)}), bf16[2,768,3072]{2,1,0:T(8,128)(2,1)}) %all-gather.39.cloned.1.call-update) | async-done | bytes 9437200 | tf_op jit(solution)/shard_map/all_gather | solution.py:32
  2714.8 117.5 %all-gather.41.cloned.1.call-done = bf16[2,3072,1536]{2,1,0:T(8,128)(2,1)} async-done(((bf16[2,768,1536]{2,1,0:T(8,128)(2,1)}), bf16[2,3072,1536]{2,1,0:T(8,128)(2,1)}) %all-gather.41.cloned.1.call-update) | async-done | bytes 18874384 | tf_op jit(solution)/shard_map/all_gather | solution.py:31
  2832.2 22.5 add_convert_fusion.7
  2854.8 116.2 %all-gather.43.cloned.1.call-done = bf16[2,768,3072]{2,1,0:T(8,128)(2,1)} async-done(((bf16[2,768,1536]{2,1,0:T(8,128)(2,1)}), bf16[2,768,3072]{2,1,0:T(8,128)(2,1)}) %all-gather.43.cloned.1.call-update) | async-done | bytes 9437200 | tf_op jit(solution)/shard_map/all_gather | solution.py:35
  2971.0 48.6 add_convert_fusion.2
  3020.1 296.5 %all-gather.45.cloned.1.call-done = bf16[2,4096,3072]{2,1,0:T(8,128)(2,1)} async-done(((bf16[2,4096,768]{2,1,0:T(8,128)(2,1)}), bf16[2,4096,3072]{2,1,0:T(8,128)(2,1)}) %all-gather.45.cloned.1.call-update) | async-done | bytes 50331664 | tf_op jit(solution)/shard_map/all_gather | solution.py:28
  3316.5 48.7 fusion.3
  3365.4 209.0 %reduce-scatter.12.cloned.1.call-done = f32[2,768,1536]{2,1,0:T(8,128)} async-done(((f32[2,768,3072]{2,1,0:T(8,128)}), f32[2,768,1536]{2,1,0:T(8,128)}) %reduce-scatter.12.cloned.1.call-update) | async-done | bytes 9437200 | tf_op jit(solution)/shard_map/reduce_scatter | solution.py:30
  3574.3 6.4 convert_element_type.138
  3581.8 115.2 %all-gather.47.cloned.1.call-done = bf16[2,768,3072]{2,1,0:T(8,128)(2,1)} async-done(((bf16[2,768,1536]{2,1,0:T(8,128)(2,1)}), bf16[2,768,3072]{2,1,0:T(8,128)(2,1)}) %all-gather.47.cloned.1.call-update) | async-done | bytes 9437200 | tf_op jit(solution)/shard_map/all_gather | solution.py:32
  3697.0 117.6 %all-gather.49.cloned.1.call-done = bf16[2,3072,1536]{2,1,0:T(8,128)(2,1)} async-done(((bf16[2,768,1536]{2,1,0:T(8,128)(2,1)}), bf16[2,3072,1536]{2,1,0:T(8,128)(2,1)}) %all-gather.49.cloned.1.call-update) | async-done | bytes 18874384 | tf_op jit(solution)/shard_map/all_gather | solution.py:31
  3814.6 22.5 add_convert_fusion.6
  3837.2 116.1 %all-gather.51.cloned.1.call-done = bf16[2,768,3072]{2,1,0:T(8,128)(2,1)} async-done(((bf16[2,768,1536]{2,1,0:T(8,128)(2,1)}), bf16[2,768,3072]{2,1,0:T(8,128)(2,1)}) %all-gather.51.cloned.1.call-update) | async-done | bytes 9437200 | tf_op jit(solution)/shard_map/all_gather | solution.py:35
  3953.3 48.6 add_convert_fusion.1
  4002.2 296.7 %all-gather.53.cloned.1.call-done = bf16[2,4096,3072]{2,1,0:T(8,128)(2,1)} async-done(((bf16[2,4096,768]{2,1,0:T(8,128)(2,1)}), bf16[2,4096,3072]{2,1,0:T(8,128)(2,1)}) %all-gather.53.cloned.1.call-update) | async-done | bytes 50331664 | tf_op jit(solution)/shard_map/all_gather | solution.py:28
  4298.9 48.7 fusion.4
  4347.7 209.0 %reduce-scatter.14.cloned.1.call-done = f32[2,768,1536]{2,1,0:T(8,128)} async-done(((f32[2,768,3072]{2,1,0:T(8,128)}), f32[2,768,1536]{2,1,0:T(8,128)}) %reduce-scatter.14.cloned.1.call-update) | async-done | bytes 9437200 | tf_op jit(solution)/shard_map/reduce_scatter | solution.py:30
  4556.7 6.4 convert_element_type.145
  4564.0 115.3 %all-gather.55.cloned.1.call-done = bf16[2,768,3072]{2,1,0:T(8,128)(2,1)} async-done(((bf16[2,768,1536]{2,1,0:T(8,128)(2,1)}), bf16[2,768,3072]{2,1,0:T(8,128)(2,1)}) %all-gather.55.cloned.1.call-update) | async-done | bytes 9437200 | tf_op jit(solution)/shard_map/all_gather | solution.py:32
  4679.3 117.5 %all-gather.57.cloned.1.call-done = bf16[2,3072,1536]{2,1,0:T(8,128)(2,1)} async-done(((bf16[2,768,1536]{2,1,0:T(8,128)(2,1)}), bf16[2,3072,1536]{2,1,0:T(8,128)(2,1)}) %all-gather.57.cloned.1.call-update) | async-done | bytes 18874384 | tf_op jit(solution)/shard_map/all_gather | solution.py:31
  4796.8 22.5 add_convert_fusion.5
  4820.7 114.9 %all-gather.59.cloned.1.call-done = bf16[2,768,3072]{2,1,0:T(8,128)(2,1)} async-done(((bf16[2,768,1536]{2,1,0:T(8,128)(2,1)}), bf16[2,768,3072]{2,1,0:T(8,128)(2,1)}) %all-gather.59.cloned.1.call-update) | async-done | bytes 9437200 | tf_op jit(solution)/shard_map/all_gather | solution.py:35
  4935.5 52.4 %multiply_subtract_fusion = f32[2,4096,768]{2,1,0:T(8,128)} fusion(f32[2,4096,768]{2,1,0:T(8,128)} %param.6, bf16[2,4096,768]{2,1,0:T(8,128)(2,1)} %add_convert_fusion.1, f32[]{:T(128)S(6)} %mul.80, f32[]{:T(128)S(6)} %sub.6, bf16[2,4096,3072]{2,1,0:T(8,128)(2,1)} %all-gather.53.cloned.1.call-done, bf16[2,768,3072]{2,1,0:T(8,128)(2,1)} %all-gather.59.cloned.1.call-done), kind=kOutput, calls=%fused_computation.2 | convolution fusion | flops 38705037312 | bytes 122683400 | tf_op jit(solution)/shard_map/erk,eck->erc/dot_general | solution.py:36
  (51 shorter events, 7.0 us)
Async XLA Ops:
  7.2 362.6 %all-gather.21.cloned.1.call-start = ((), (), s32[]{:S(2)}) async-start(), calls=%async_computation.5 | async-start | bytes 62914560 | tf_op jit(solution)/shard_map/all_gather | solution.py:28
  72.0 555.5 %reduce-scatter.6.cloned.1.call-start = ((), (), s32[]{:S(2)}) async-start(), calls=%async_computation.6 | async-start | bytes 28311552 | tf_op jit(solution)/shard_map/reduce_scatter | solution.py:30
  418.5 331.7 %all-gather.23.cloned.1.call-start = ((), (), s32[]{:S(2)}) async-start(), calls=%async_computation.7 | async-start | bytes 14155776 | tf_op jit(solution)/shard_map/all_gather | solution.py:32
  634.0 233.7 %all-gather.25.cloned.1.call-start = ((), (), s32[]{:S(2)}) async-start(), calls=%async_computation.8 | async-start | bytes 23592960 | tf_op jit(solution)/shard_map/all_gather | solution.py:31
  634.6 371.8 %all-gather.27.cloned.1.call-start = ((), (), s32[]{:S(2)}) async-start(), calls=%async_computation.9 | async-start | bytes 14155776 | tf_op jit(solution)/shard_map/all_gather | solution.py:35
  890.2 461.7 %all-gather.29.cloned.1.call-start = ((), (), s32[]{:S(2)}) async-start(), calls=%async_computation.10 | async-start | bytes 62914560 | tf_op jit(solution)/shard_map/all_gather | solution.py:28
  1055.1 554.7 %reduce-scatter.8.cloned.1.call-start = ((), (), s32[]{:S(2)}) async-start(), calls=%async_computation.11 | async-start | bytes 28311552 | tf_op jit(solution)/shard_map/reduce_scatter | solution.py:30
  1400.7 331.7 %all-gather.31.cloned.1.call-start = ((), (), s32[]{:S(2)}) async-start(), calls=%async_computation.12 | async-start | bytes 14155776 | tf_op jit(solution)/shard_map/all_gather | solution.py:32
  1616.2 233.8 %all-gather.33.cloned.1.call-start = ((), (), s32[]{:S(2)}) async-start(), calls=%async_computation.13 | async-start | bytes 23592960 | tf_op jit(solution)/shard_map/all_gather | solution.py:31
  1617.0 371.8 %all-gather.35.cloned.1.call-start = ((), (), s32[]{:S(2)}) async-start(), calls=%async_computation.14 | async-start | bytes 14155776 | tf_op jit(solution)/shard_map/all_gather | solution.py:35
  1872.6 461.8 %all-gather.37.cloned.1.call-start = ((), (), s32[]{:S(2)}) async-start(), calls=%async_computation.15 | async-start | bytes 62914560 | tf_op jit(solution)/shard_map/all_gather | solution.py:28
  2037.4 554.7 %reduce-scatter.10.cloned.1.call-start = ((), (), s32[]{:S(2)}) async-start(), calls=%async_computation.16 | async-start | bytes 28311552 | tf_op jit(solution)/shard_map/reduce_scatter | solution.py:30
  2383.1 331.7 %all-gather.39.cloned.1.call-start = ((), (), s32[]{:S(2)}) async-start(), calls=%async_computation.17 | async-start | bytes 14155776 | tf_op jit(solution)/shard_map/all_gather | solution.py:32
  2598.6 233.7 %all-gather.41.cloned.1.call-start = ((), (), s32[]{:S(2)}) async-start(), calls=%async_computation.18 | async-start | bytes 23592960 | tf_op jit(solution)/shard_map/all_gather | solution.py:31
  2599.2 371.8 %all-gather.43.cloned.1.call-start = ((), (), s32[]{:S(2)}) async-start(), calls=%async_computation.19 | async-start | bytes 14155776 | tf_op jit(solution)/shard_map/all_gather | solution.py:35
  2854.8 461.8 %all-gather.45.cloned.1.call-start = ((), (), s32[]{:S(2)}) async-start(), calls=%async_computation.20 | async-start | bytes 62914560 | tf_op jit(solution)/shard_map/all_gather | solution.py:28
  3019.6 554.7 %reduce-scatter.12.cloned.1.call-start = ((), (), s32[]{:S(2)}) async-start(), calls=%async_computation.21 | async-start | bytes 28311552 | tf_op jit(solution)/shard_map/reduce_scatter | solution.py:30
  3365.3 331.7 %all-gather.47.cloned.1.call-start = ((), (), s32[]{:S(2)}) async-start(), calls=%async_computation.22 | async-start | bytes 14155776 | tf_op jit(solution)/shard_map/all_gather | solution.py:32
  3580.8 233.8 %all-gather.49.cloned.1.call-start = ((), (), s32[]{:S(2)}) async-start(), calls=%async_computation.23 | async-start | bytes 23592960 | tf_op jit(solution)/shard_map/all_gather | solution.py:31
  3581.6 371.8 %all-gather.51.cloned.1.call-start = ((), (), s32[]{:S(2)}) async-start(), calls=%async_computation.24 | async-start | bytes 14155776 | tf_op jit(solution)/shard_map/all_gather | solution.py:35
  3837.2 461.7 %all-gather.53.cloned.1.call-start = ((), (), s32[]{:S(2)}) async-start(), calls=%async_computation.25 | async-start | bytes 62914560 | tf_op jit(solution)/shard_map/all_gather | solution.py:28
  4002.0 554.7 %reduce-scatter.14.cloned.1.call-start = ((), (), s32[]{:S(2)}) async-start(), calls=%async_computation.26 | async-start | bytes 28311552 | tf_op jit(solution)/shard_map/reduce_scatter | solution.py:30
  4347.6 331.7 %all-gather.55.cloned.1.call-start = ((), (), s32[]{:S(2)}) async-start(), calls=%async_computation.27 | async-start | bytes 14155776 | tf_op jit(solution)/shard_map/all_gather | solution.py:32
  4563.1 233.7 %all-gather.57.cloned.1.call-start = ((), (), s32[]{:S(2)}) async-start(), calls=%async_computation.28 | async-start | bytes 23592960 | tf_op jit(solution)/shard_map/all_gather | solution.py:31
  4563.7 371.8 %all-gather.59.cloned.1.call-start = ((), (), s32[]{:S(2)}) async-start(), calls=%async_computation.29 | async-start | bytes 14155776 | tf_op jit(solution)/shard_map/all_gather | solution.py:35
Sparse Core Ops, SparseCore 0:
  72.2 297.5 all-gather.20
  418.6 208.8 reduce-scatter.5
  634.1 116.0 all-gather.22
  752.2 115.4 all-gather.24
  890.4 116.0 all-gather.26
  1055.2 296.7 all-gather.28
  1400.8 208.8 reduce-scatter.7
  1616.3 116.0 all-gather.30
  1734.5 115.4 all-gather.32
  1872.7 116.0 all-gather.34
  2037.5 296.7 all-gather.36
  2383.2 208.8 reduce-scatter.9
  2598.7 116.0 all-gather.38
  2716.7 115.4 all-gather.40
  2854.9 116.0 all-gather.42
  3019.7 296.7 all-gather.44
  3365.4 208.8 reduce-scatter.11
  3580.9 116.0 all-gather.46
  3699.1 115.4 all-gather.48
  3837.3 116.0 all-gather.50
  4002.1 296.7 all-gather.52
  4347.8 208.8 reduce-scatter.13
  4563.3 116.0 all-gather.54
  4681.3 115.4 all-gather.56
  4819.5 115.9 all-gather.58
where the time goes:
time: 5000 us; the launch traced here: 4990 us
  waiting for transfers between devices  4280 us (86%)
  matrix products  603 us (12%)
  other arithmetic  71.4 us (1%)
    all_gather x5, waiting for transfers between devices, local_step(): x_rows = lax.all_gather(x_iter, 'tp', axis=2, tiled=True)  1480 us
    reduce_scatter x5, waiting for transfers between devices, local_step(): lax.psum_scatter(gram_part, 'fsdp', scatter_dimension=2, tiled=True)  1040 us
    all_gather x5, waiting for transfers between devices, local_step(): gram_cols = lax.all_gather(gram_blk, 'tp', axis=1, tiled=True)  588 us
    all_gather x5, waiting for transfers between devices, local_step(): poly_rows = lax.all_gather(poly_blk, 'fsdp', axis=2, tiled=True)  579 us
    all_gather x5, waiting for transfers between devices, local_step(): gram_rows = lax.all_gather(gram_blk, 'fsdp', axis=2, tiled=True)  576 us
    dot_general x5, matrix products, local_step(): jnp.einsum('erk,eck->erc', x_rows, poly_rows, preferred_element_type=jnp....  247 us
    dot_general x5, matrix products, local_step(): jnp.einsum('erc,erd->ecd', x_iter, x_rows, preferred_element_type=jnp.flo...  244 us
    dot_general x5, matrix products, local_step(): jnp.einsum('eab,ebc->eac', gram_rows, gram_cols, preferred_element_type=j...  113 us
  transfers between devices with their start and end apart: 25, of which 25 were waited for; matrix products, arithmetic and copies ran while one was open for 0% of the time, Pallas kernels for 0%

commit v1 on v0

v1 whole, which is shorter than its diff:
```python
import functools
import math

import jax
import jax.numpy as jnp
from jax import lax
from jax.experimental import pallas as pl
from jax.experimental.pallas import tpu as pltpu
from jax.sharding import PartitionSpec as P

NS_STEPS = 5
COEF_A = 3.4445
COEF_B = -4.7750
COEF_C = 2.0315
NORM_EPS = 1e-7

MESH = pl.DeviceIdType.MESH
F32 = jnp.float32
BF16 = jnp.bfloat16

BLK = 512
VMEM_LIMIT = 64 * 1024 * 1024 - 65536


def here():
    fsdp = lax.axis_index('fsdp')
    tp = lax.axis_index('tp')
    return fsdp, tp, tp // 2, tp % 2


def tri_index(step, num_blk):
    step = jnp.asarray(step, jnp.int32)
    row = jnp.int32(0)
    start = jnp.int32(0)
    first = 0
    for blk in range(1, num_blk):
        first += num_blk - blk + 1
        past = (step >= first).astype(jnp.int32)
        row = row + past
        start = start + past * (num_blk - blk + 1)
    return row, step - start + row


def dot_tn(lhs, rhs):
    return lax.dot_general(lhs, rhs, (((0,), (0,)), ((), ())), preferred_element_type=F32)


def spread_kernel(rows, cols, x_ref, out_ref, stage_ref, send_sem, recv_sem, loc_sem):
    fsdp, tp, chip, core = here()
    barrier = pltpu.get_barrier_semaphore()
    targets = []
    for off in range(8):
        far_f = (fsdp + off // 4) % 2
        far_x = (chip + (off // 2) % 2) % 2
        far_c = (core + off % 2) % 2
        targets.append((far_f, far_x, far_c))
    for off in range(1, 8):
        far_f, far_x, far_c = targets[off]
        pl.semaphore_signal(barrier, inc=1, device_id={'fsdp': far_f, 'tp': 2 * far_x + far_c}, device_id_type=MESH)
    pl.semaphore_wait(barrier, 7)

    def piece(off):
        far_f, far_x, far_c = targets[off]
        mat = (far_f + far_x) % 2
        src = x_ref.at[mat, pl.ds(pl.multiple_of(far_c * rows, rows), rows), :]
        dst = out_ref.at[pl.ds(pl.multiple_of(fsdp * rows, rows), rows), pl.ds(pl.multiple_of(tp * cols, cols), cols)]
        return src, dst

    copies = []
    for off in (6, 7, 2, 3, 4, 5, 1):
        far_f, far_x, far_c = targets[off]
        src, dst = piece(off)
        copy = pltpu.make_async_remote_copy(
            src_ref=src, dst_ref=dst, send_sem=send_sem.at[off], recv_sem=recv_sem.at[off],
            device_id={'fsdp': far_f, 'tp': 2 * far_x + far_c}, device_id_type=MESH)
        copy.start()
        copies.append(copy)
    src, dst = piece(0)
    to_vmem = pltpu.make_async_copy(src, stage_ref, loc_sem.at[0])
    to_vmem.start()
    to_vmem.wait()
    to_hbm = pltpu.make_async_copy(stage_ref, dst, loc_sem.at[1])
    to_hbm.start()
    to_hbm.wait()
    for copy in copies:
        copy.wait()


def spread(x_loc):
    _, rows, cols = x_loc.shape
    rows = rows // 2
    return pl.pallas_call(
        functools.partial(spread_kernel, rows, cols),
        out_shape=jax.ShapeDtypeStruct((2 * rows, 4 * cols), BF16),
        in_specs=[pl.BlockSpec(memory_space=pl.ANY)],
        out_specs=pl.BlockSpec(memory_space=pl.ANY),
        scratch_shapes=[
            pltpu.VMEM((rows, cols), BF16),
            pltpu.SemaphoreType.DMA((8,)),
            pltpu.SemaphoreType.DMA((8,)),
            pltpu.SemaphoreType.DMA((2,)),
        ],
        compiler_params=pltpu.CompilerParams(collective_id=0, has_side_effects=True, vmem_limit_bytes=VMEM_LIMIT),
        name='spread',
    )(x_loc)


def poly_kernel(num_blk, xi_ref, xj_ref, b_ref, a_ref, part_ref, got_ref, stage_ref,
                psend, precv, asend, arecv, bloc, bsend, brecv):
    total = num_blk * (num_blk + 1) // 2
    step = pl.program_id(0)
    _, tp, chip, core = here()
    peer = {'tp': 2 * chip + 1 - core}

    @pl.when(step == 0)
    def _():
        barrier = pltpu.get_barrier_semaphore()
        pl.semaphore_signal(barrier, inc=1, device_id=peer, device_id_type=MESH)
        pl.semaphore_wait(barrier, 1)

    def rows_of(blk):
        return pl.ds(pl.multiple_of(blk * BLK, BLK), BLK)

    def part_copy(num):
        return pltpu.make_async_remote_copy(
            src_ref=part_ref.at[num % 2], dst_ref=got_ref.at[num // 2], send_sem=psend.at[num], recv_sem=precv.at[num],
            device_id=peer, device_id_type=MESH)

    def a_copy(num, flip):
        row, col = tri_index(num, num_blk)
        if flip:
            row, col = col, row
        ref = a_ref.at[col, rows_of(row), :]
        return pltpu.make_async_remote_copy(
            src_ref=ref, dst_ref=ref, send_sem=asend.at[flip, num], recv_sem=arecv.at[flip, num],
            device_id=peer, device_id_type=MESH)

    def finish(num):
        row, col = tri_index(num, num_blk)
        part_copy(num).wait_recv()
        val = part_ref[num % 2] + got_ref[num // 2]
        a_ref[col, rows_of(row), :] = val.astype(BF16)
        a_copy(num, 0).start()

        @pl.when(row != col)
        def _():
            a_ref[row, rows_of(col), :] = val.T.astype(BF16)
            a_copy(num, 1).start()

    part_ref[step % 2] = dot_tn(xi_ref[...], xj_ref[...])
    mine = (step + core) % 2 == 0
    theirs = (step + core) % 2 == 1

    @pl.when(theirs)
    def _():
        part_copy(step).start()

    @pl.when(jnp.logical_and(step >= 1, theirs))
    def _():
        finish(step - 1)

    @pl.when(jnp.logical_and(step >= 1, mine))
    def _():
        part_copy(step - 1).wait_send()

    @pl.when(step == total - 1)
    def _():
        @pl.when(mine)
        def _():
            finish(total - 1)

        @pl.when(theirs)
        def _():
            part_copy(total - 1).wait_send()

        num_mine = (total + 1) // 2 - (total % 2) * core
        num_theirs = total // 2 + (total % 2) * core

        def wait_sent(k, _):
            num = 2 * k + core
            row, col = tri_index(num, num_blk)
            a_copy(num, 0).wait_send()

            @pl.when(row != col)
            def _():
                a_copy(num, 1).wait_send()
            return 0

        def wait_got(k, _):
            num = 2 * k + 1 - core
            row, col = tri_index(num, num_blk)
            a_copy(num, 0).wait_recv()

            @pl.when(row != col)
            def _():
                a_copy(num, 1).wait_recv()
            return 0

        lax.fori_loop(0, num_theirs, wait_got, 0)
        lax.fori_loop(0, num_mine, wait_sent, 0)

        def b_copies(num, flip):
            slot = (num // 2) % 2
            row, col = tri_index(num, num_blk)
            if flip:
                row, col = col, row
            src = stage_ref.at[slot, flip]
            dst = b_ref.at[rows_of(row), rows_of(col)]
            local = pltpu.make_async_copy(src, dst, bloc.at[flip, num])
            remote = pltpu.make_async_remote_copy(
                src_ref=src, dst_ref=dst, send_sem=bsend.at[flip, num], recv_sem=brecv.at[flip, num],
                device_id=peer, device_id_type=MESH)
            return local, remote

        def b_drain(num):
            row, col = tri_index(num, num_blk)
            local, remote = b_copies(num, 0)
            local.wait()
            remote.wait_send()

            @pl.when(row != col)
            def _():
                local, remote = b_copies(num, 1)
                local.wait()
                remote.wait_send()

        def square(k, _):
            num = 2 * k + core
            row, col = tri_index(num, num_blk)
            slot = k % 2

            @pl.when(k >= 2)
            def _():
                b_drain(num - 4)

            gram_sq = dot_tn(a_ref[row], a_ref[col]).astype(BF16)
            gram = a_ref[col, rows_of(row), :]
            poly = COEF_B * gram.astype(F32) + COEF_C * gram_sq.astype(F32)
            stage_ref[slot, 0] = poly.astype(BF16)
            local, remote = b_copies(num, 0)
            remote.start()
            local.start()

            @pl.when(row != col)
            def _():
                stage_ref[slot, 1] = poly.T.astype(BF16)
                local, remote = b_copies(num, 1)
                remote.start()
                local.start()
            return 0

        lax.fori_loop(0, num_mine, square, 0)
        b_drain(2 * (num_mine - 2) + core)
        b_drain(2 * (num_mine - 1) + core)

        def wait_b(k, _):
            num = 2 * k + 1 - core
            row, col = tri_index(num, num_blk)
            b_copies(num, 0)[1].wait_recv()

            @pl.when(row != col)
            def _():
                b_copies(num, 1)[1].wait_recv()
            return 0

        lax.fori_loop(0, num_theirs, wait_b, 0)


def poly(x_mat):
    rows, cols = x_mat.shape
    num_blk = cols // BLK
    total = num_blk * (num_blk + 1) // 2
    half = (total + 1) // 2
    dma = pltpu.SemaphoreType.DMA
    return pl.pallas_call(
        functools.partial(poly_kernel, num_blk),
        grid=(total,),
        out_shape=jax.ShapeDtypeStruct((cols, cols), BF16),
        in_specs=[
            pl.BlockSpec((rows, BLK), lambda s: (0, tri_index(s, num_blk)[0])),
            pl.BlockSpec((rows, BLK), lambda s: (0, tri_index(s, num_blk)[1])),
        ],
        out_specs=pl.BlockSpec(memory_space=pl.ANY),
        scratch_shapes=[
            pltpu.VMEM((num_blk, cols, BLK), BF16),
            pltpu.VMEM((2, BLK, BLK), F32),
            pltpu.VMEM((half, BLK, BLK), F32),
            pltpu.VMEM((2, 2, BLK, BLK), BF16),
            dma((total,)), dma((total,)),
            dma((2, total)), dma((2, total)),
            dma((2, total)), dma((2, total)), dma((2, total)),
        ],
        compiler_params=pltpu.CompilerParams(
            collective_id=1, has_side_effects=True, vmem_limit_bytes=VMEM_LIMIT, dimension_semantics=('arbitrary',)),
        name='poly',
    )(x_mat, x_mat)


def update_kernel(tile, x_ref, b_ref, out_ref):
    blk = pl.program_id(0)
    upd = jnp.dot(x_ref[...], b_ref[...], preferred_element_type=F32)
    x_old = x_ref[:, pl.ds(pl.multiple_of(blk * tile, tile), tile)]
    out_ref[...] = (COEF_A * x_old.astype(F32) + upd).astype(BF16)


def update(x_mat, b_mat, row_tile=512, col_tile=1024):
    rows, cols = x_mat.shape
    return pl.pallas_call(
        functools.partial(update_kernel, col_tile),
        grid=(cols // col_tile, rows // row_tile),
        out_shape=jax.ShapeDtypeStruct((rows, cols), BF16),
        in_specs=[
            pl.BlockSpec((row_tile, cols), lambda j, i: (i, 0)),
            pl.BlockSpec((cols, col_tile), lambda j, i: (0, j)),
        ],
        out_specs=pl.BlockSpec((row_tile, col_tile), lambda j, i: (i, j)),
        compiler_params=pltpu.CompilerParams(
            vmem_limit_bytes=VMEM_LIMIT, dimension_semantics=('arbitrary', 'arbitrary')),
        name='update',
    )(x_mat, b_mat)


def last_kernel(tile, tab_ref, x_ref, b_ref, out_ref):
    blk = tab_ref[1, pl.program_id(0)]
    upd = jnp.dot(x_ref[...], b_ref[...], preferred_element_type=F32)
    x_old = x_ref[:, pl.ds(pl.multiple_of(blk * tile, tile), tile)]
    out_ref[0] = (COEF_A * x_old.astype(F32) + upd).astype(BF16)


def last_update(x_mat, b_mat, table, row_tile=512):
    rows, cols = x_mat.shape
    half, tile = rows // 2, cols // 4
    per = half // row_tile
    return pl.pallas_call(
        functools.partial(last_kernel, tile),
        grid_spec=pltpu.PrefetchScalarGridSpec(
            num_scalar_prefetch=1,
            grid=(4, per),
            in_specs=[
                pl.BlockSpec((row_tile, cols), lambda p, i, tab: (tab[0, p] * per + i, 0)),
                pl.BlockSpec((cols, tile), lambda p, i, tab: (0, tab[1, p])),
            ],
            out_specs=pl.BlockSpec((1, row_tile, tile), lambda p, i, tab: (p, i, 0)),
        ),
        out_shape=jax.ShapeDtypeStruct((4, half, tile), BF16),
        compiler_params=pltpu.CompilerParams(
            vmem_limit_bytes=VMEM_LIMIT, dimension_semantics=('arbitrary', 'arbitrary')),
        name='last_update',
    )(table, x_mat, b_mat)


def collect_kernel(rows, in_ref, out_ref, stage_ref, send_sem, recv_sem, loc_sem):
    fsdp, tp, chip, core = here()
    mat = (fsdp + chip) % 2
    peers = [
        {'fsdp': fsdp, 'tp': 2 * (1 - chip)},
        {'fsdp': 1 - fsdp, 'tp': 2 * chip + 1},
        {'fsdp': fsdp, 'tp': 2 * chip + 1 - core},
    ]
    far = [{'fsdp': fsdp * (1 - core) + (1 - fsdp) * core, 'tp': 2 * (chip * core + (1 - chip) * (1 - core)) + k} for k in (0, 1)]
    barrier = pltpu.get_barrier_semaphore()
    for dev in far + [peers[2]]:
        pl.semaphore_signal(barrier, inc=1, device_id=dev, device_id_type=MESH)
    pl.semaphore_wait(barrier, 3)

    def dst(which):
        return out_ref.at[which, pl.ds(pl.multiple_of(core * rows, rows), rows), :]

    def copy(num):
        return pltpu.make_async_remote_copy(
            src_ref=in_ref.at[num], dst_ref=dst(mat), send_sem=send_sem.at[num],
            recv_sem=recv_sem.at[core if num < 2 else 2], device_id=peers[num], device_id_type=MESH)

    copies = [copy(num) for num in range(3)]
    for item in copies:
        item.start()
    to_vmem = pltpu.make_async_copy(in_ref.at[3], stage_ref, loc_sem.at[0])
    to_vmem.start()
    to_vmem.wait()
    to_hbm = pltpu.make_async_copy(stage_ref, dst(mat), loc_sem.at[1])
    to_hbm.start()
    to_hbm.wait()
    for item in copies:
        item.wait_send()
    for k in (0, 1):
        pltpu.make_async_remote_copy(
            src_ref=in_ref.at[0], dst_ref=out_ref.at[1 - mat, pl.ds(k * rows, rows), :], send_sem=send_sem.at[0],
            recv_sem=recv_sem.at[k], device_id=far[k], device_id_type=MESH).wait_recv()
    pltpu.make_async_remote_copy(
        src_ref=in_ref.at[2], dst_ref=out_ref.at[mat, pl.ds(pl.multiple_of((1 - core) * rows, rows), rows), :],
        send_sem=send_sem.at[2], recv_sem=recv_sem.at[2], device_id=peers[2], device_id_type=MESH).wait_recv()


def collect(pieces):
    _, rows, cols = pieces.shape
    dma = pltpu.SemaphoreType.DMA
    return pl.pallas_call(
        functools.partial(collect_kernel, rows),
        out_shape=jax.ShapeDtypeStruct((2, 2 * rows, cols), BF16),
        in_specs=[pl.BlockSpec(memory_space=pl.ANY)],
        out_specs=pl.BlockSpec(memory_space=pl.ANY),
        scratch_shapes=[pltpu.VMEM((rows, cols), BF16), dma((3,)), dma((3,)), dma((2,))],
        compiler_params=pltpu.CompilerParams(collective_id=2, has_side_effects=True, vmem_limit_bytes=VMEM_LIMIT),
        name='collect',
    )(pieces)


def solution(mesh):
    fsdp_size = mesh.shape['fsdp']
    mat_spec = P('stage', 'fsdp', 'tp')
    scalar_spec = P()

    def local_step(weight, momentum, gradient, learn_rate, mom_coef, weight_decay):
        row_dim = weight.shape[1] * fsdp_size
        fsdp, tp, chip, core = here()
        grad_full = gradient.astype(F32)
        mom_new = mom_coef * momentum + grad_full
        nesterov = grad_full + mom_coef * mom_new
        sq_sum = lax.psum(jnp.sum(nesterov * nesterov, axis=(1, 2)), ('fsdp', 'tp'))
        norm_val = jnp.sqrt(sq_sum)[:, None, None]
        x_loc = (nesterov / (norm_val + NORM_EPS)).astype(BF16)
        x_mat = spread(x_loc)
        for _ in range(NS_STEPS - 1):
            x_mat = update(x_mat, poly(x_mat))
        row_half = jnp.stack([fsdp, 1 - fsdp, fsdp, fsdp])
        col_quarter = jnp.stack([2 * (1 - chip), 2 * chip + 1, 2 * chip + 1 - core, 2 * chip + core])
        table = jnp.stack([row_half, col_quarter]).astype(jnp.int32)
        x_fin = collect(last_update(x_mat, poly(x_mat), table))
        step_scale = learn_rate * 0.2 * math.sqrt(row_dim)
        new_weight = (1.0 - learn_rate * weight_decay) * weight - step_scale * x_fin.astype(F32)
        return new_weight, mom_new

    return jax.shard_map(local_step, mesh=mesh, in_specs=(mat_spec,) * 3 + (scalar_spec,) * 3, out_specs=(mat_spec, mat_spec), check_vma=False)
```

time: 5000 us -> 1300 us (0.26)
  waiting for transfers between devices: 4280 us -> 0 us
  Pallas kernels: 0 us -> 1210 us
  matrix products: 603 us -> 0 us
    all_gather x20 -> x0, waiting for transfers between devices: 3230 us -> none  [the longest x5 1480 us: local_step(): x_rows = lax.all_gather(x_iter, 'tp', axis=2, tiled=True)]
    pallas_call x0 -> x12, Pallas kernels: none -> 1210 us  [the longest x5 460 us: poly(): pl.pallas_call(functools.partial(poly_kernel, num_blk), grid=(total,), ou...]
    reduce_scatter x5 -> x0, waiting for transfers between devices: 1040 us -> none  [local_step(): lax.psum_scatter(gram_part, 'fsdp', scatter_dimension=2, tiled=True)]
    dot_general x15 -> x0, matrix products: 603 us -> none  [the longest x5 247 us: local_step(): jnp.einsum('erk,eck->erc', x_rows, poly_rows, preferred_element_type=jnp....]
  transfers between devices with their start and end apart: 25 -> 0, of which waited for: 25 -> 0; matrix products, arithmetic and copies ran while one was open for 0% -> 0% of each run, Pallas kernels for 0% -> 0%
where the time goes in v1:
time: 1300 us
  Pallas kernels  1210 us (93%)
  other arithmetic  60.8 us (5%)
  blocking collectives  25 us (2%)
    pallas_call x5, Pallas kernels, poly(): pl.pallas_call(functools.partial(poly_kernel, num_blk), grid=(total,), ou...  460 us
    pallas_call x4, Pallas kernels, update(): pl.pallas_call(functools.partial(update_kernel, col_tile), grid=(cols //...  355 us
    pallas_call x1, Pallas kernels, spread(): pl.pallas_call(functools.partial(spread_kernel, rows, cols), out_shape=ja...  274 us
    pallas_call x1, Pallas kernels, collect(): pl.pallas_call(functools.partial(collect_kernel, rows), out_shape=jax.Sha...  71.2 us
    pallas_call x1, Pallas kernels, last_update(): pl.pallas_call(functools.partial(last_kernel, tile), grid_spec=pltpu.Pref...  49 us

profile of v1, /device:TPU:0, one launch (start us, length us, event | category | flops | bytes accessed | tf_op | source)
XLA Modules:
  0.0 1298.3 jit_solution(16013962814450085723)
XLA Ops:
  1.3 21.5 %multiply_reduce_fusion = (f32[2]{0:T(128)S(1)}, f32[2,4096,768]{2,1,0:T(8,128)}) fusion(bf16[2,4096,768]{2,1,0:T(8,128)(2,1)} %param.8, f32[]{:T(128)S(6)} %copy.9, f32[2,4096,768]{2,1,0:T(8,128)} %param.7), kind=kLoop, calls=%fused_computation.4 | loop fusion | flops 44040192 | bytes 62914572 | tf_op jit(solution)/shard_map/reduce_sum | solution.py:419
  22.8 25.0 %psum.7 = f32[2]{0:T(128)S(1)} all-reduce(f32[2]{0:T(128)S(1)} %get-tuple-element.2), channel_id=1, replica_groups=mesh['stage'=1,'fsdp'=2,'tp'=4] {'fsdp','tp'}, use_global_device_ids=true, to_apply=%region_1.2 | all-reduce | flops 2 | bytes 16 | tf_op jit(solution)/shard_map/psum | solution.py:419
  47.8 17.4 %divide_convert_fusion.x_ref = bf16[2,4096,768]{2,1,0:T(8,128)(2,1)} fusion(f32[2,4096,768]{2,1,0:T(8,128)} %get-tuple-element.3, bf16[2,4096,768]{2,1,0:T(8,128)(2,1)} %param.8, f32[2]{0:T(128)S(1)} %sqrt_add_fusion, f32[]{:T(128)S(6)} %copy.9), kind=kLoop, calls=%fused_computation.3 | loop fusion | flops 31457280 | bytes 50331660 | tf_op jit(solution)/shard_map/convert_element_type | solution.py:421
  65.2 274.5 %spread.1.xi_ref.xj_ref.x_ref = bf16[4096,3072]{1,0:T(8,128)(2,1)} custom-call(bf16[2,4096,768]{2,1,0:T(8,128)(2,1)} %divide_convert_fusion.x_ref), custom_call_target="tpu_custom_call" | custom-call | tf_op jit(solution)/shard_map/spread/pallas_call | solution.py:92
  339.7 92.0 %poly.5.b_ref = bf16[3072,3072]{1,0:T(8,128)(2,1)} custom-call(bf16[4096,3072]{1,0:T(8,128)(2,1)} %spread.1.xi_ref.xj_ref.x_ref, bf16[4096,3072]{1,0:T(8,128)(2,1)} %spread.1.xi_ref.xj_ref.x_ref), custom_call_target="tpu_custom_call" | custom-call | tf_op jit(solution)/shard_map/poly/pallas_call | solution.py:275
  431.7 88.7 %update.4.xi_ref.xj_ref.x_ref = bf16[4096,3072]{1,0:T(8,128)(2,1)} custom-call(bf16[4096,3072]{1,0:T(8,128)(2,1)} %spread.1.xi_ref.xj_ref.x_ref, bf16[3072,3072]{1,0:T(8,128)(2,1)} %poly.5.b_ref), custom_call_target="tpu_custom_call" | custom-call | tf_op jit(solution)/shard_map/update/pallas_call | solution.py:308
  520.3 92.2 %poly.6.b_ref = bf16[3072,3072]{1,0:T(8,128)(2,1)} custom-call(bf16[4096,3072]{1,0:T(8,128)(2,1)} %update.4.xi_ref.xj_ref.x_ref, bf16[4096,3072]{1,0:T(8,128)(2,1)} %update.4.xi_ref.xj_ref.x_ref), custom_call_target="tpu_custom_call" | custom-call | tf_op jit(solution)/shard_map/poly/pallas_call | solution.py:275
  612.5 88.9 %update.5.xi_ref.xj_ref.x_ref = bf16[4096,3072]{1,0:T(8,128)(2,1)} custom-call(bf16[4096,3072]{1,0:T(8,128)(2,1)} %update.4.xi_ref.xj_ref.x_ref, bf16[3072,3072]{1,0:T(8,128)(2,1)} %poly.6.b_ref), custom_call_target="tpu_custom_call" | custom-call | tf_op jit(solution)/shard_map/update/pallas_call | solution.py:308
  701.4 91.8 %poly.7.b_ref = bf16[3072,3072]{1,0:T(8,128)(2,1)} custom-call(bf16[4096,3072]{1,0:T(8,128)(2,1)} %update.5.xi_ref.xj_ref.x_ref, bf16[4096,3072]{1,0:T(8,128)(2,1)} %update.5.xi_ref.xj_ref.x_ref), custom_call_target="tpu_custom_call" | custom-call | tf_op jit(solution)/shard_map/poly/pallas_call | solution.py:275
  793.3 88.7 %update.6.xi_ref.xj_ref.x_ref = bf16[4096,3072]{1,0:T(8,128)(2,1)} custom-call(bf16[4096,3072]{1,0:T(8,128)(2,1)} %update.5.xi_ref.xj_ref.x_ref, bf16[3072,3072]{1,0:T(8,128)(2,1)} %poly.7.b_ref), custom_call_target="tpu_custom_call" | custom-call | tf_op jit(solution)/shard_map/update/pallas_call | solution.py:308
  881.9 92.4 %poly.8.b_ref = bf16[3072,3072]{1,0:T(8,128)(2,1)} custom-call(bf16[4096,3072]{1,0:T(8,128)(2,1)} %update.6.xi_ref.xj_ref.x_ref, bf16[4096,3072]{1,0:T(8,128)(2,1)} %update.6.xi_ref.xj_ref.x_ref), custom_call_target="tpu_custom_call" | custom-call | tf_op jit(solution)/shard_map/poly/pallas_call | solution.py:275
  974.3 88.7 %update.7.xi_ref.xj_ref.x_ref = bf16[4096,3072]{1,0:T(8,128)(2,1)} custom-call(bf16[4096,3072]{1,0:T(8,128)(2,1)} %update.6.xi_ref.xj_ref.x_ref, bf16[3072,3072]{1,0:T(8,128)(2,1)} %poly.8.b_ref), custom_call_target="tpu_custom_call" | custom-call | tf_op jit(solution)/shard_map/update/pallas_call | solution.py:308
  1063.1 91.8 %poly.9.b_ref = bf16[3072,3072]{1,0:T(8,128)(2,1)} custom-call(bf16[4096,3072]{1,0:T(8,128)(2,1)} %update.7.xi_ref.xj_ref.x_ref, bf16[4096,3072]{1,0:T(8,128)(2,1)} %update.7.xi_ref.xj_ref.x_ref), custom_call_target="tpu_custom_call" | custom-call | tf_op jit(solution)/shard_map/poly/pallas_call | solution.py:275
  1154.9 0.1 add_bitcast_fusion
  1155.0 0.6 pad_add_fusion.tab_ref
  1155.6 49.0 %last_update.1.in_ref = bf16[4,2048,768]{2,1,0:T(8,128)(2,1)} custom-call(s32[2,4]{1,0:T(2,128)} %pad_add_fusion.tab_ref, bf16[4096,3072]{1,0:T(8,128)(2,1)} %update.7.xi_ref.xj_ref.x_ref, bf16[3072,3072]{1,0:T(8,128)(2,1)} %poly.9.b_ref), custom_call_target="tpu_custom_call" | custom-call | tf_op jit(solution)/shard_map/last_update/pallas_call | solution.py:334
  1204.6 71.2 %collect.1 = bf16[2,4096,768]{2,1,0:T(8,128)(2,1)} custom-call(bf16[4,2048,768]{2,1,0:T(8,128)(2,1)} %last_update.1.in_ref), custom_call_target="tpu_custom_call" | custom-call | tf_op jit(solution)/shard_map/collect/pallas_call | solution.py:397
  1277.1 21.2 %multiply_subtract_fusion = f32[2,4096,768]{2,1,0:T(8,128)} fusion(bf16[2,4096,768]{2,1,0:T(8,128)(2,1)} %collect.1, f32[2,4096,768]{2,1,0:T(8,128)} %param.6, f32[]{:T(128)S(6)} %mul.43, f32[]{:T(128)S(6)} %sub.19), kind=kLoop, calls=%fused_computation.2 | loop fusion | flops 25165824 | bytes 62914568 | tf_op jit(solution)/shard_map/sub | solution.py:430
  (1 shorter events, 0.0 us)

commit v2 on v0

v2 whole, which is shorter than its diff:
```python
import functools
import math

import jax
import jax.numpy as jnp
from jax import lax
from jax.experimental import pallas as pl
from jax.experimental.pallas import tpu as pltpu
from jax.sharding import PartitionSpec as P


NS_STEPS = 5
COEF_A = 3.4445
COEF_B = -4.7750
COEF_C = 2.0315
NORM_EPS = 1e-7


MESH = pl.DeviceIdType.MESH
F32 = jnp.float32
BF16 = jnp.bfloat16

BLK = 512
VMEM_LIMIT = 64 * 1024 * 1024 - 65536


def here():
    fsdp = lax.axis_index('fsdp')
    tp = lax.axis_index('tp')
    return fsdp, tp, tp // 2, tp % 2


def tri_index(step, num_blk):
    step = jnp.asarray(step, jnp.int32)
    row = jnp.int32(0)
    start = jnp.int32(0)
    first = 0
    for blk in range(1, num_blk):
        first += num_blk - blk + 1
        past = (step >= first).astype(jnp.int32)
        row = row + past
        start = start + past * (num_blk - blk + 1)
    return row, step - start + row


def dot_tn(lhs, rhs):
    return lax.dot_general(lhs, rhs, (((0,), (0,)), ((), ())), preferred_element_type=F32)


CHUNK = 512


def spread_kernel(rows, cols, mu_ref, sq_ref, m_ref, g_ref, out_ref, all_ref, m_buf, g_buf, x_buf,
                  load_sem, nsend, nrecv, send_sem, recv_sem):
    fsdp, tp, chip, core = here()
    me = 4 * fsdp + tp
    per = rows // CHUNK
    steps = 4 * per
    chips = ((0, 1), (1, 0), (1, 1), (0, 0))

    def device(hop, flip):
        far_f = (fsdp + chips[hop][0]) % 2
        far_x = (chip + chips[hop][1]) % 2
        far_c = (core + flip) % 2
        return far_f, 2 * far_x + far_c

    others = [(hop, flip) for hop in range(4) for flip in range(2) if (hop, flip) != (3, 0)]

    def m_load(mat, first, slot):
        return pltpu.make_async_copy(m_ref.at[mat, pl.ds(first, CHUNK), :], m_buf.at[slot], load_sem.at[0, slot])

    def g_load(mat, first, slot):
        return pltpu.make_async_copy(g_ref.at[mat, pl.ds(first, CHUNK), :], g_buf.at[slot], load_sem.at[1, slot])

    def where(step):
        near = step // (2 * per)
        flip = (step // per) % 2
        quarter = step % per
        mat = (fsdp + chip + 1 - near) % 2
        far_c = (core + flip) % 2
        first = pl.multiple_of(far_c * rows + quarter * CHUNK, CHUNK)
        return near, flip, quarter, mat, first

    def load(step, slot):
        _, _, _, mat, first = where(step)
        m_load(mat, first, slot).start()
        g_load(mat, first, slot).start()

    load(0, 0)
    barrier = pltpu.get_barrier_semaphore()
    for hop, flip in others:
        far_f, far_t = device(hop, flip)
        pl.semaphore_signal(barrier, inc=1, device_id={'fsdp': far_f, 'tp': far_t}, device_id_type=MESH)
    pl.semaphore_wait(barrier, 7)

    all_ref[me] = sq_ref[...]
    norm_copies = []
    for num, (hop, flip) in enumerate(others):
        far_f, far_t = device(hop, flip)
        copy = pltpu.make_async_remote_copy(
            src_ref=sq_ref, dst_ref=all_ref.at[me], send_sem=nsend.at[num], recv_sem=nrecv.at[num],
            device_id={'fsdp': far_f, 'tp': far_t}, device_id_type=MESH)
        copy.start()
        norm_copies.append(copy)
    for copy in norm_copies:
        copy.wait()
    total = all_ref[0]
    for dev in range(1, 8):
        total = total + all_ref[dev]
    norm = jnp.sqrt(total) + NORM_EPS
    mu = mu_ref[0]

    def x_copy(hop, flip, step, quarter):
        far_f, _ = device(hop, 0)
        far_x = (chip + chips[hop][1]) % 2
        far_t = 2 * far_x + (core + flip) % 2
        dst = out_ref.at[pl.ds(pl.multiple_of(fsdp * rows + quarter * CHUNK, CHUNK), CHUNK),
                         pl.ds(pl.multiple_of(tp * cols, cols), cols)]
        return pltpu.make_async_remote_copy(
            src_ref=x_buf.at[step], dst_ref=dst, send_sem=send_sem.at[hop, flip, quarter],
            recv_sem=recv_sem.at[hop, flip, quarter], device_id={'fsdp': far_f, 'tp': far_t}, device_id_type=MESH)

    def own_copy(step, quarter):
        dst = out_ref.at[pl.ds(pl.multiple_of(fsdp * rows + quarter * CHUNK, CHUNK), CHUNK),
                         pl.ds(pl.multiple_of(tp * cols, cols), cols)]
        return pltpu.make_async_copy(x_buf.at[step], dst, send_sem.at[3, 0, quarter])

    def make(step, _):
        near, flip, quarter, mat, first = where(step)
        slot = step % 2
        m_load(mat, first, slot).wait()
        g_load(mat, first, slot).wait()

        @pl.when(step + 1 < steps)
        def _():
            load(step + 1, 1 - slot)

        grad = g_buf[slot].astype(F32)
        nesterov = grad + mu * (mu * m_buf[slot] + grad)
        scale = jnp.where(mat == 0, norm[0:1, 0:1], norm[1:2, 0:1])
        x_buf[step] = (nesterov / scale).astype(BF16)

        @pl.when(near == 0)
        def _():
            x_copy(0, flip, step, quarter).start()
            x_copy(1, flip, step, quarter).start()

        @pl.when(near == 1)
        def _():
            x_copy(2, flip, step, quarter).start()

            @pl.when(flip == 1)
            def _():
                x_copy(3, flip, step, quarter).start()

            @pl.when(flip == 0)
            def _():
                own_copy(step, quarter).start()

        return 0

    lax.fori_loop(0, steps, make, 0)
    for quarter in range(per):
        own_copy(2 * per + quarter, quarter).wait()
        for hop, flip in others:
            step = (hop // 2) * 2 * per + flip * per + quarter
            x_copy(hop, flip, step, quarter).wait()


def spread(mu, sq_sum, momentum, gradient):
    mats, rows, cols = momentum.shape
    rows = rows // 2
    dma = pltpu.SemaphoreType.DMA
    per = rows // CHUNK
    sq_tile = jnp.zeros((8, 128), F32).at[:mats].set(sq_sum[:, None])
    return pl.pallas_call(
        functools.partial(spread_kernel, rows, cols),
        out_shape=jax.ShapeDtypeStruct((2 * rows, 4 * cols), BF16),
        in_specs=[
            pl.BlockSpec(memory_space=pltpu.SMEM),
            pl.BlockSpec(memory_space=pltpu.VMEM),
            pl.BlockSpec(memory_space=pl.ANY),
            pl.BlockSpec(memory_space=pl.ANY),
        ],
        out_specs=pl.BlockSpec(memory_space=pl.ANY),
        scratch_shapes=[
            pltpu.VMEM((8, 8, 128), F32),
            pltpu.VMEM((2, CHUNK, cols), F32),
            pltpu.VMEM((2, CHUNK, cols), BF16),
            pltpu.VMEM((4 * per, CHUNK, cols), BF16),
            dma((2, 2)), dma((7,)), dma((7,)),
            dma((4, 2, per)), dma((4, 2, per)),
        ],
        compiler_params=pltpu.CompilerParams(collective_id=0, has_side_effects=True, vmem_limit_bytes=VMEM_LIMIT),
        name='spread',
    )(mu.reshape(1), sq_tile, momentum, gradient)


def poly_kernel(num_blk, x_hbm, b_ref, x_ref, a_ref, part_ref, got_ref, stage_ref,
                xsem, psend, precv, asend, arecv, bloc, bsend, brecv):
    total = num_blk * (num_blk + 1) // 2
    _, _, chip, core = here()
    peer = {'tp': 2 * chip + 1 - core}

    def x_load(blk):
        return pltpu.make_async_copy(
            x_hbm.at[:, pl.ds(pl.multiple_of(blk * BLK, BLK), BLK)], x_ref.at[blk], xsem.at[blk])

    for blk in range(num_blk):
        x_load(blk).start()
    barrier = pltpu.get_barrier_semaphore()
    pl.semaphore_signal(barrier, inc=1, device_id=peer, device_id_type=MESH)
    pl.semaphore_wait(barrier, 1)

    def rows_of(blk):
        return pl.ds(pl.multiple_of(blk * BLK, BLK), BLK)

    def part_copy(num):
        return pltpu.make_async_remote_copy(
            src_ref=part_ref.at[num % 2], dst_ref=got_ref.at[num // 2], send_sem=psend.at[num], recv_sem=precv.at[num],
            device_id=peer, device_id_type=MESH)

    def a_copy(num, flip):
        row, col = tri_index(num, num_blk)
        if flip:
            row, col = col, row
        ref = a_ref.at[col, rows_of(row), :]
        return pltpu.make_async_remote_copy(
            src_ref=ref, dst_ref=ref, send_sem=asend.at[flip, num], recv_sem=arecv.at[flip, num],
            device_id=peer, device_id_type=MESH)

    def finish(num):
        row, col = tri_index(num, num_blk)
        part_copy(num).wait_recv()
        val = part_ref[num % 2] + got_ref[num // 2]
        a_ref[col, rows_of(row), :] = val.astype(BF16)
        a_copy(num, 0).start()

        @pl.when(row != col)
        def _():
            a_ref[row, rows_of(col), :] = val.T.astype(BF16)
            a_copy(num, 1).start()

    def gram(step, _):
        row, col = tri_index(step, num_blk)

        @pl.when(row == 0)
        def _():
            x_load(col).wait()

        part_ref[step % 2] = dot_tn(x_ref[row], x_ref[col])
        mine = (step + core) % 2 == 0
        theirs = (step + core) % 2 == 1

        @pl.when(theirs)
        def _():
            part_copy(step).start()

        @pl.when(jnp.logical_and(step >= 1, theirs))
        def _():
            finish(step - 1)

        @pl.when(jnp.logical_and(step >= 1, mine))
        def _():
            part_copy(step - 1).wait_send()

        return 0

    lax.fori_loop(0, total, gram, 0)
    last_mine = (total - 1 + core) % 2 == 0
    last_theirs = (total - 1 + core) % 2 == 1

    @pl.when(last_mine)
    def _():
        finish(total - 1)

    @pl.when(last_theirs)
    def _():
        part_copy(total - 1).wait_send()

    num_mine = (total + 1) // 2 - (total % 2) * core
    num_theirs = total // 2 + (total % 2) * core

    def wait_sent(k, _):
        num = 2 * k + core
        row, col = tri_index(num, num_blk)
        a_copy(num, 0).wait_send()

        @pl.when(row != col)
        def _():
            a_copy(num, 1).wait_send()

        return 0

    def wait_got(k, _):
        num = 2 * k + 1 - core
        row, col = tri_index(num, num_blk)
        a_copy(num, 0).wait_recv()

        @pl.when(row != col)
        def _():
            a_copy(num, 1).wait_recv()

        return 0

    lax.fori_loop(0, num_theirs, wait_got, 0)
    lax.fori_loop(0, num_mine, wait_sent, 0)

    def b_copies(num, flip):
        slot = (num // 2) % 2
        row, col = tri_index(num, num_blk)
        if flip:
            row, col = col, row
        src = stage_ref.at[slot, flip]
        dst = b_ref.at[rows_of(row), rows_of(col)]
        local = pltpu.make_async_copy(src, dst, bloc.at[flip, num])
        remote = pltpu.make_async_remote_copy(
            src_ref=src, dst_ref=dst, send_sem=bsend.at[flip, num], recv_sem=brecv.at[flip, num],
            device_id=peer, device_id_type=MESH)
        return local, remote

    def b_drain(num):
        row, col = tri_index(num, num_blk)
        local, remote = b_copies(num, 0)
        local.wait()
        remote.wait_send()

        @pl.when(row != col)
        def _():
            local, remote = b_copies(num, 1)
            local.wait()
            remote.wait_send()

    def square(k, _):
        num = 2 * k + core
        row, col = tri_index(num, num_blk)
        slot = k % 2

        @pl.when(k >= 2)
        def _():
            b_drain(num - 4)

        gram_sq = dot_tn(a_ref[row], a_ref[col]).astype(BF16)
        gram = a_ref[col, rows_of(row), :]
        poly = COEF_B * gram.astype(F32) + COEF_C * gram_sq.astype(F32)
        stage_ref[slot, 0] = poly.astype(BF16)
        local, remote = b_copies(num, 0)
        remote.start()
        local.start()

        @pl.when(row != col)
        def _():
            stage_ref[slot, 1] = poly.T.astype(BF16)
            local, remote = b_copies(num, 1)
            remote.start()
            local.start()

        return 0

    lax.fori_loop(0, num_mine, square, 0)
    b_drain(2 * (num_mine - 2) + core)
    b_drain(2 * (num_mine - 1) + core)

    def wait_b(k, _):
        num = 2 * k + 1 - core
        row, col = tri_index(num, num_blk)
        b_copies(num, 0)[1].wait_recv()

        @pl.when(row != col)
        def _():
            b_copies(num, 1)[1].wait_recv()

        return 0

    lax.fori_loop(0, num_theirs, wait_b, 0)


def poly(x_mat):
    rows, cols = x_mat.shape
    num_blk = cols // BLK
    total = num_blk * (num_blk + 1) // 2
    half = (total + 1) // 2
    dma = pltpu.SemaphoreType.DMA
    return pl.pallas_call(
        functools.partial(poly_kernel, num_blk),
        out_shape=jax.ShapeDtypeStruct((cols, cols), BF16),
        in_specs=[pl.BlockSpec(memory_space=pl.ANY)],
        out_specs=pl.BlockSpec(memory_space=pl.ANY),
        scratch_shapes=[
            pltpu.VMEM((num_blk, rows, BLK), BF16),
            pltpu.VMEM((num_blk, cols, BLK), BF16),
            pltpu.VMEM((2, BLK, BLK), F32),
            pltpu.VMEM((half, BLK, BLK), F32),
            pltpu.VMEM((2, 2, BLK, BLK), BF16),
            dma((num_blk,)), dma((total,)), dma((total,)),
            dma((2, total)), dma((2, total)),
            dma((2, total)), dma((2, total)), dma((2, total)),
        ],
        compiler_params=pltpu.CompilerParams(
            collective_id=1, has_side_effects=True, vmem_limit_bytes=VMEM_LIMIT),
        name='poly',
    )(x_mat)


def update_kernel(tile, x_ref, b_ref, out_ref):
    blk = pl.program_id(0)
    upd = jnp.dot(x_ref[...], b_ref[...], preferred_element_type=F32)
    x_old = x_ref[:, pl.ds(pl.multiple_of(blk * tile, tile), tile)]
    out_ref[...] = (COEF_A * x_old.astype(F32) + upd).astype(BF16)


def update(x_mat, b_mat, row_tile=1024, col_tile=1024):
    rows, cols = x_mat.shape
    return pl.pallas_call(
        functools.partial(update_kernel, col_tile),
        grid=(cols // col_tile, rows // row_tile),
        out_shape=jax.ShapeDtypeStruct((rows, cols), BF16),
        in_specs=[
            pl.BlockSpec((row_tile, cols), lambda j, i: (i, 0)),
            pl.BlockSpec((cols, col_tile), lambda j, i: (0, j)),
        ],
        out_specs=pl.BlockSpec((row_tile, col_tile), lambda j, i: (i, j)),
        compiler_params=pltpu.CompilerParams(
            vmem_limit_bytes=VMEM_LIMIT, dimension_semantics=('arbitrary', 'arbitrary')),
        name='update',
    )(x_mat, b_mat)


def pair_kernel(tile, base, tab_ref, x_ref, b_ref, out0_ref, out1_ref):
    which = pl.program_id(0)
    blk = tab_ref[1, base + which]
    upd = jnp.dot(x_ref[...], b_ref[...], preferred_element_type=F32)
    x_old = x_ref[:, pl.ds(pl.multiple_of(blk * tile, tile), tile)]
    val = (COEF_A * x_old.astype(F32) + upd).astype(BF16)

    @pl.when(which == 0)
    def _():
        out0_ref[...] = val

    @pl.when(which == 1)
    def _():
        out1_ref[...] = val


def last_pieces(x_mat, b_mat, table, base, piece_rows, row_tile=1024):
    _, cols = x_mat.shape
    tile = cols // 4
    last = piece_rows // row_tile - 1
    return pl.pallas_call(
        functools.partial(pair_kernel, tile, base),
        grid_spec=pltpu.PrefetchScalarGridSpec(
            num_scalar_prefetch=1,
            grid=(2, last + 1),
            in_specs=[
                pl.BlockSpec((row_tile, cols), lambda p, i, tab: (tab[0, base + p] + i, 0)),
                pl.BlockSpec((cols, tile), lambda p, i, tab: (0, tab[1, base + p])),
            ],
            out_specs=[
                pl.BlockSpec((row_tile, tile), lambda p, i, tab: (i * (1 - p) + last * p, 0)),
                pl.BlockSpec((row_tile, tile), lambda p, i, tab: (i * p, 0)),
            ],
        ),
        out_shape=[jax.ShapeDtypeStruct((piece_rows, tile), BF16)] * 2,
        compiler_params=pltpu.CompilerParams(
            vmem_limit_bytes=VMEM_LIMIT, dimension_semantics=('arbitrary', 'arbitrary')),
        cost_estimate=pl.CostEstimate(
            flops=4 * piece_rows * tile * cols, bytes_accessed=4 * cols * (piece_rows + tile), transcendentals=0),
        name='last_pieces',
    )(table, x_mat, b_mat)


def apply_kernel(tab_ref, scale_ref, w_ref, x_ref, *rest):
    rest[-1][0] = scale_ref[0] * w_ref[0] - scale_ref[1] * x_ref[...].astype(F32)


def apply_piece(weight, x_piece, scales, table, base, so_far, row_tile=512):
    rows, cols = x_piece.shape
    extra = [] if so_far is None else [so_far]
    w_spec = pl.BlockSpec((1, row_tile, cols), lambda i, tab: (tab[0, base], tab[1, base] + i, 0))
    return pl.pallas_call(
        apply_kernel,
        grid_spec=pltpu.PrefetchScalarGridSpec(
            num_scalar_prefetch=1,
            grid=(rows // row_tile,),
            in_specs=[
                pl.BlockSpec(memory_space=pltpu.SMEM),
                w_spec,
                pl.BlockSpec((row_tile, cols), lambda i, tab: (i, 0)),
            ] + [pl.BlockSpec(memory_space=pl.ANY)] * len(extra),
            out_specs=w_spec,
        ),
        out_shape=jax.ShapeDtypeStruct(weight.shape, F32),
        input_output_aliases={4: 0} if extra else {},
        compiler_params=pltpu.CompilerParams(vmem_limit_bytes=VMEM_LIMIT, dimension_semantics=('arbitrary',)),
        cost_estimate=pl.CostEstimate(flops=3 * rows * cols, bytes_accessed=10 * rows * cols, transcendentals=0),
        name='apply_piece',
    )(table, scales, weight, x_piece, *extra)


def solution(mesh):
    fsdp_size = mesh.shape['fsdp']
    mat_spec = P('stage', 'fsdp', 'tp')
    scalar_spec = P()

    def local_step(weight, momentum, gradient, learn_rate, mom_coef, weight_decay):
        row_dim = weight.shape[1] * fsdp_size
        fsdp, _, chip, core = here()
        grad_full = gradient.astype(F32)
        mom_new = mom_coef * momentum + grad_full
        nesterov = grad_full + mom_coef * mom_new
        sq_sum = jnp.sum(nesterov * nesterov, axis=(1, 2))
        sub = row_dim // 4
        half = sub // 2
        mat = (fsdp + chip) % 2
        far = 1 - mat
        r_here, r_far = fsdp * (sub // 1024), (1 - fsdp) * (sub // 1024)
        step = half // 1024
        x_col, y_col = 2 * (1 - chip) + core, 2 * chip + 1 - core
        piece_tab = jnp.stack([
            jnp.stack([r_here, r_far, r_here + step, r_far + step, r_here, r_here]),
            jnp.stack([x_col, y_col, x_col, y_col, y_col, 2 * chip + core]),
        ]).astype(jnp.int32)
        c_here, c_far = core * (sub // 512), (1 - core) * (sub // 512)
        step = half // 512
        apply_tab = jnp.stack([
            jnp.stack([mat, mat, far, far, far, far]),
            jnp.stack([c_here, c_far, c_here, c_far, c_here + step, c_far + step]),
        ]).astype(jnp.int32)
        scales = jnp.stack([1.0 - learn_rate * weight_decay, learn_rate * 0.2 * math.sqrt(row_dim)])
        sq_sum, piece_tab, apply_tab, scales = lax.optimization_barrier((sq_sum, piece_tab, apply_tab, scales))
        x_mat = spread(mom_coef, sq_sum, momentum, gradient)
        for _ in range(NS_STEPS - 1):
            x_mat = update(x_mat, poly(x_mat))
        b_mat = poly(x_mat)

        def permute(piece, kind):
            pairs = []
            for src in range(8):
                f_src, t_src = src // 4, src % 4
                if kind == 'x':
                    dst = f_src * 4 + (t_src + 2) % 4
                elif kind == 'y':
                    dst = (1 - f_src) * 4 + t_src + 1 - 2 * (t_src % 2)
                else:
                    dst = f_src * 4 + t_src + 1 - 2 * (t_src % 2)
                pairs.append((src, dst))
            return lax.ppermute(piece, ('fsdp', 'tp'), pairs)

        moved = []
        tie = b_mat
        for part in range(2):
            to_x, to_y = last_pieces(x_mat, tie, piece_tab, 2 * part, half)
            moved.append(permute(to_x, 'x'))
            moved.append(permute(to_y, 'y'))
            tie, _, _ = lax.optimization_barrier((tie, to_x, to_y))
        near, own = last_pieces(x_mat, tie, piece_tab, 4, sub)
        near = permute(near, 'core')
        new_weight = apply_piece(weight, own, scales, apply_tab, 0, None)
        new_weight = apply_piece(weight, near, scales, apply_tab, 1, new_weight)
        for num, x_piece in enumerate(moved):
            new_weight = apply_piece(weight, x_piece, scales, apply_tab, 2 + num, new_weight)
        return new_weight, mom_new

    return jax.shard_map(local_step, mesh=mesh, in_specs=(mat_spec,) * 3 + (scalar_spec,) * 3, out_specs=(mat_spec, mat_spec), check_vma=False)
```

time: 5000 us -> 1230 us (0.25)
  waiting for transfers between devices: 4280 us -> 43.4 us
  Pallas kernels: 0 us -> 1150 us
  matrix products: 603 us -> 0 us
    all_gather x20 -> x0, waiting for transfers between devices: 3230 us -> none  [the longest x5 1480 us: local_step(): x_rows = lax.all_gather(x_iter, 'tp', axis=2, tiled=True)]
    pallas_call x0 -> x19, Pallas kernels: none -> 1150 us  [the longest x5 429 us: poly(): pl.pallas_call(functools.partial(poly_kernel, num_blk), out_shape=jax.Sha...]
    reduce_scatter x5 -> x0, waiting for transfers between devices: 1040 us -> none  [local_step(): lax.psum_scatter(gram_part, 'fsdp', scatter_dimension=2, tiled=True)]
    dot_general x15 -> x0, matrix products: 603 us -> none  [the longest x5 247 us: local_step(): jnp.einsum('erk,eck->erc', x_rows, poly_rows, preferred_element_type=jnp....]
  transfers between devices with their start and end apart: 25 -> 5, of which waited for: 25 -> 2; matrix products, arithmetic and copies ran while one was open for 0% -> 0% of each run, Pallas kernels for 0% -> 2%
where the time goes in v2:
time: 1230 us; the launch traced here: 1220 us
  Pallas kernels  1150 us (93%)
  waiting for transfers between devices  43.4 us (4%)
  other arithmetic  22.7 us (2%)
    pallas_call x5, Pallas kernels, poly(): pl.pallas_call(functools.partial(poly_kernel, num_blk), out_shape=jax.Sha...  429 us
    pallas_call x4, Pallas kernels, update(): pl.pallas_call(functools.partial(update_kernel, col_tile), grid=(cols //...  344 us
    pallas_call x1, Pallas kernels, spread(): pl.pallas_call(functools.partial(spread_kernel, rows, cols), out_shape=ja...  281 us
    pallas_call x3, Pallas kernels, last_pieces(): pl.pallas_call(functools.partial(pair_kernel, tile, base), grid_spec=pltp...  61.7 us
    ppermute x5, waiting for transfers between devices, permute(): return lax.ppermute(piece, ('fsdp', 'tp'), pairs)  43.4 us
    pallas_call x6, Pallas kernels, apply_piece(): pl.pallas_call(apply_kernel, grid_spec=pltpu.PrefetchScalarGridSpec(num_s...  32.2 us
  transfers between devices with their start and end apart: 5, of which 2 were waited for; matrix products, arithmetic and copies ran while one was open for 0% of the time, Pallas kernels for 2%

profile of v2, /device:TPU:0, one launch (start us, length us, event | category | flops | bytes accessed | tf_op | source)
XLA Modules:
  0.0 1222.5 jit_solution(17076038378122144754)
XLA Ops:
  2.6 0.7 pad_maximum_fusion.scale_ref
  3.3 0.1 stack.103
  3.4 0.1 stack.98
  3.4 21.5 %fusion.1 = (f32[2]{0:T(128)S(1)}, f32[2,4096,768]{2,1,0:T(8,128)}) fusion(bf16[2,4096,768]{2,1,0:T(8,128)(2,1)} %g_ref.1, f32[]{:T(128)} %copy.19, f32[2,4096,768]{2,1,0:T(8,128)} %m_ref.1), kind=kLoop, calls=%fused_computation.3 | loop fusion | flops 44040192 | bytes 62914572 | tf_op jit(solution)/shard_map/reduce_sum | solution.py:511
  25.0 0.1 stack.93
  25.0 0.1 stack.109
  25.1 0.6 pad_add_fusion
  25.7 0.7 scatter.8.sq_ref
  26.3 281.2 %spread.1.x_hbm.x_ref = bf16[4096,3072]{1,0:T(8,128)(2,1)} custom-call(f32[1]{0:T(128)} %bitcast.20.mu_ref, f32[8,128]{1,0:T(8,128)} %scatter.8.sq_ref, f32[2,4096,768]{2,1,0:T(8,128)} %m_ref.1, bf16[2,4096,768]{2,1,0:T(8,128)(2,1)} %g_ref.1), custom_call_target="tpu_custom_call" | custom-call | tf_op jit(solution)/shard_map/spread/pallas_call | solution.py:176
  307.6 85.8 %poly.5.b_ref = bf16[3072,3072]{1,0:T(8,128)(2,1)} custom-call(bf16[4096,3072]{1,0:T(8,128)(2,1)} %spread.1.x_hbm.x_ref), custom_call_target="tpu_custom_call" | custom-call | tf_op jit(solution)/shard_map/poly/pallas_call | solution.py:384
  393.4 86.0 %update.4.x_hbm.x_ref = bf16[4096,3072]{1,0:T(8,128)(2,1)} custom-call(bf16[4096,3072]{1,0:T(8,128)(2,1)} %spread.1.x_hbm.x_ref, bf16[3072,3072]{1,0:T(8,128)(2,1)} %poly.5.b_ref), custom_call_target="tpu_custom_call" | custom-call | tf_op jit(solution)/shard_map/update/pallas_call | solution.py:414
  479.5 85.7 %poly.6.b_ref = bf16[3072,3072]{1,0:T(8,128)(2,1)} custom-call(bf16[4096,3072]{1,0:T(8,128)(2,1)} %update.4.x_hbm.x_ref), custom_call_target="tpu_custom_call" | custom-call | tf_op jit(solution)/shard_map/poly/pallas_call | solution.py:384
  565.2 86.2 %update.5.x_hbm.x_ref = bf16[4096,3072]{1,0:T(8,128)(2,1)} custom-call(bf16[4096,3072]{1,0:T(8,128)(2,1)} %update.4.x_hbm.x_ref, bf16[3072,3072]{1,0:T(8,128)(2,1)} %poly.6.b_ref), custom_call_target="tpu_custom_call" | custom-call | tf_op jit(solution)/shard_map/update/pallas_call | solution.py:414
  651.4 85.7 %poly.7.b_ref = bf16[3072,3072]{1,0:T(8,128)(2,1)} custom-call(bf16[4096,3072]{1,0:T(8,128)(2,1)} %update.5.x_hbm.x_ref), custom_call_target="tpu_custom_call" | custom-call | tf_op jit(solution)/shard_map/poly/pallas_call | solution.py:384
  737.1 86.0 %update.6.x_hbm.x_ref = bf16[4096,3072]{1,0:T(8,128)(2,1)} custom-call(bf16[4096,3072]{1,0:T(8,128)(2,1)} %update.5.x_hbm.x_ref, bf16[3072,3072]{1,0:T(8,128)(2,1)} %poly.7.b_ref), custom_call_target="tpu_custom_call" | custom-call | tf_op jit(solution)/shard_map/update/pallas_call | solution.py:414
  823.2 85.7 %poly.8.b_ref = bf16[3072,3072]{1,0:T(8,128)(2,1)} custom-call(bf16[4096,3072]{1,0:T(8,128)(2,1)} %update.6.x_hbm.x_ref), custom_call_target="tpu_custom_call" | custom-call | tf_op jit(solution)/shard_map/poly/pallas_call | solution.py:384
  908.9 86.2 %update.7.x_hbm.x_ref = bf16[4096,3072]{1,0:T(8,128)(2,1)} custom-call(bf16[4096,3072]{1,0:T(8,128)(2,1)} %update.6.x_hbm.x_ref, bf16[3072,3072]{1,0:T(8,128)(2,1)} %poly.8.b_ref), custom_call_target="tpu_custom_call" | custom-call | tf_op jit(solution)/shard_map/update/pallas_call | solution.py:414
  995.1 85.7 %poly.9.b_ref = bf16[3072,3072]{1,0:T(8,128)(2,1)} custom-call(bf16[4096,3072]{1,0:T(8,128)(2,1)} %update.7.x_hbm.x_ref), custom_call_target="tpu_custom_call" | custom-call | tf_op jit(solution)/shard_map/poly/pallas_call | solution.py:384
  1080.9 17.0 %last_pieces.3 = (bf16[1024,768]{1,0:T(8,128)(2,1)}, bf16[1024,768]{1,0:T(8,128)(2,1)}) custom-call(s32[2,6]{1,0:T(2,128)} %get-tuple-element.28.tab_ref, bf16[4096,3072]{1,0:T(8,128)(2,1)} %update.7.x_hbm.x_ref, bf16[3072,3072]{1,0:T(8,128)(2,1)} %poly.9.b_ref), custom_call_target="tpu_custom_call" | custom-call | flops 9663676416 | bytes 22020096 | tf_op jit(solution)/shard_map/last_pieces/pallas_call | solution.py:449
  1097.8 16.9 %last_pieces.4 = (bf16[1024,768]{1,0:T(8,128)(2,1)}, bf16[1024,768]{1,0:T(8,128)(2,1)}) custom-call(s32[2,6]{1,0:T(2,128)} %get-tuple-element.28.tab_ref, bf16[4096,3072]{1,0:T(8,128)(2,1)} %update.7.x_hbm.x_ref, bf16[3072,3072]{1,0:T(8,128)(2,1)} %poly.9.b_ref), custom_call_target="tpu_custom_call" | custom-call | flops 9663676416 | bytes 22020096 | tf_op jit(solution)/shard_map/last_pieces/pallas_call | solution.py:449
  1114.7 27.8 %last_pieces.5 = (bf16[2048,768]{1,0:T(8,128)(2,1)}, bf16[2048,768]{1,0:T(8,128)(2,1)}) custom-call(s32[2,6]{1,0:T(2,128)} %get-tuple-element.28.tab_ref, bf16[4096,3072]{1,0:T(8,128)(2,1)} %update.7.x_hbm.x_ref, bf16[3072,3072]{1,0:T(8,128)(2,1)} %poly.9.b_ref), custom_call_target="tpu_custom_call" | custom-call | flops 19327352832 | bytes 34603008 | tf_op jit(solution)/shard_map/last_pieces/pallas_call | solution.py:449
  1142.5 0.5 collective-permute-start.4
  1143.1 0.4 collective-permute-start.3
  1143.4 0.3 collective-permute-start.2
  1143.8 1.3 collective-permute-start.1
  1145.1 1.5 collective-permute-start
  1146.6 7.3 apply_piece.6.rest_0_
  1153.9 0.0 collective-permute-done.4.x_ref
  1153.9 7.4 apply_piece.7.rest_0_
  1161.3 19.4 %collective-permute-done.3.x_ref = bf16[1024,768]{1,0:T(8,128)(2,1)} collective-permute-done((bf16[1024,768]{1,0:T(8,128)(2,1)}, bf16[1024,768]{1,0:T(8,128)(2,1)}, u32[]{:S(2)}, u32[]{:S(2)}) %collective-permute-start.3) | collective-permute-done | bytes 1572896 | tf_op jit(solution)/shard_map/ppermute | solution.py:547
  1180.6 4.4 apply_piece.8.rest_0_
  1185.0 0.0 collective-permute-done.2.x_ref
  1185.0 4.4 apply_piece.9.rest_0_
  1189.4 24.0 %collective-permute-done.1.x_ref = bf16[1024,768]{1,0:T(8,128)(2,1)} collective-permute-done((bf16[1024,768]{1,0:T(8,128)(2,1)}, bf16[1024,768]{1,0:T(8,128)(2,1)}, u32[]{:S(2)}, u32[]{:S(2)}) %collective-permute-start.1) | collective-permute-done | bytes 1572896 | tf_op jit(solution)/shard_map/ppermute | solution.py:547
  1213.4 4.4 apply_piece.10.rest_0_
  1217.8 0.0 collective-permute-done.x_ref
  1217.8 4.4 apply_piece.11
  (1 shorter events, 0.0 us)
Async XLA Ops:
  1142.5 11.4 collective-permute-start.4
  1143.1 37.6 %collective-permute-start.3 = (bf16[1024,768]{1,0:T(8,128)(2,1)}, bf16[1024,768]{1,0:T(8,128)(2,1)}, u32[]{:S(2)}, u32[]{:S(2)}) collective-permute-start(bf16[1024,768]{1,0:T(8,128)(2,1)} %get-tuple-element.30), channel_id=1, source_target_pairs={{0,2},{1,3},{2,0},{3,1},{4,6},{5,7},{6,4},{7,5}} | collective-permute-start | bytes 4718600 | tf_op jit(solution)/shard_map/ppermute | solution.py:547
  1143.4 41.6 %collective-permute-start.2 = (bf16[1024,768]{1,0:T(8,128)(2,1)}, bf16[1024,768]{1,0:T(8,128)(2,1)}, u32[]{:S(2)}, u32[]{:S(2)}) collective-permute-start(bf16[1024,768]{1,0:T(8,128)(2,1)} %get-tuple-element.31), channel_id=1, source_target_pairs={{0,5},{1,4},{2,7},{3,6},{4,1},{5,0},{6,3},{7,2}} | collective-permute-start | bytes 4718600 | tf_op jit(solution)/shard_map/ppermute | solution.py:547
  1143.8 69.6 %collective-permute-start.1 = (bf16[1024,768]{1,0:T(8,128)(2,1)}, bf16[1024,768]{1,0:T(8,128)(2,1)}, u32[]{:S(2)}, u32[]{:S(2)}) collective-permute-start(bf16[1024,768]{1,0:T(8,128)(2,1)} %get-tuple-element.34), channel_id=1, source_target_pairs={{0,2},{1,3},{2,0},{3,1},{4,6},{5,7},{6,4},{7,5}} | collective-permute-start | bytes 4718600 | tf_op jit(solution)/shard_map/ppermute | solution.py:547
  1145.1 72.7 %collective-permute-start = (bf16[1024,768]{1,0:T(8,128)(2,1)}, bf16[1024,768]{1,0:T(8,128)(2,1)}, u32[]{:S(2)}, u32[]{:S(2)}) collective-permute-start(bf16[1024,768]{1,0:T(8,128)(2,1)} %get-tuple-element.33), channel_id=1, source_target_pairs={{0,5},{1,4},{2,7},{3,6},{4,1},{5,0},{6,3},{7,2}} | collective-permute-start | bytes 4718600 | tf_op jit(solution)/shard_map/ppermute | solution.py:547

commit v3 on v2

--- a/solution.py
+++ b/solution.py
@@ -196,204 +196,252 @@
     )(mu.reshape(1), sq_tile, momentum, gradient)
 
 
-def poly_kernel(num_blk, x_hbm, b_ref, x_ref, a_ref, part_ref, got_ref, stage_ref,
-                xsem, psend, precv, asend, arecv, bloc, bsend, brecv):
-    total = num_blk * (num_blk + 1) // 2
-    _, _, chip, core = here()
-    peer = {'tp': 2 * chip + 1 - core}
-
-    def x_load(blk):
+NUM_BLK = 6
+SPLIT = 5
+STEPS = NUM_BLK * (NUM_BLK + 1) // 2 - SPLIT
+HALF = STEPS // 2
+
+
+def poly_kernel(x_hbm, b_ref, x_ref, a_ref, part_ref, own_ref, sq_ref, got_ref, stage_ref,
+                xsem, psend, precv, asend, arecv, csend, crecv, fsend, frecv, bloc, bsend, brecv):
+    total = NUM_BLK * (NUM_BLK + 1) // 2
+    side, _, chip, core = here()
+    peer = {'fsdp': side, 'tp': 2 * chip + 1 - core}
+    twin = {'fsdp': 1 - side, 'tp': 2 * (1 - chip) + core}
+
+    def x_load(pos):
+        blk = pos + side * (4 * int(pos == 1) - int(pos > 1))
         return pltpu.make_async_copy(
-            x_hbm.at[:, pl.ds(pl.multiple_of(blk * BLK, BLK), BLK)], x_ref.at[blk], xsem.at[blk])
-
-    for blk in range(num_blk):
-        x_load(blk).start()
+            x_hbm.at[:, pl.ds(pl.multiple_of(blk * BLK, BLK), BLK)], x_ref.at[blk], xsem.at[pos])
+
+    for pos in range(NUM_BLK):
+        x_load(pos).start()
     barrier = pltpu.get_barrier_semaphore()
-    pl.semaphore_signal(barrier, inc=1, device_id=peer, device_id_type=MESH)
-    pl.semaphore_wait(barrier, 1)
+    for dev in (peer, twin):
+        pl.semaphore_signal(barrier, inc=1, device_id=dev, device_id_type=MESH)
+    pl.semaphore_wait(barrier, 2)
 
     def rows_of(blk):
         return pl.ds(pl.multiple_of(blk * BLK, BLK), BLK)
 
-    def part_copy(num):
+    def block(step, whose=None):
+        whose = side if whose is None else whose
+        early = (step < SPLIT) * jnp.int32(1)
+        return tri_index(step + SPLIT * (early * whose + 1 - early), NUM_BLK)
+
+    def copy_to(dev, src, dst, send, recv):
         return pltpu.make_async_remote_copy(
-            src_ref=part_ref.at[num % 2], dst_ref=got_ref.at[num // 2], send_sem=psend.at[num], recv_sem=precv.at[num],
-            device_id=peer, device_id_type=MESH)
-
-    def a_copy(num, flip):
-        row, col = tri_index(num, num_blk)
+            src_ref=src, dst_ref=dst, send_sem=send, recv_sem=recv, device_id=dev, device_id_type=MESH)
+
+    def part_copy(step):
+        return copy_to(peer, part_ref, got_ref.at[step // 2], psend.at[step], precv.at[step])
+
+    def region(row, col, flip):
+        return a_ref.at[row, rows_of(col), :] if flip else a_ref.at[col, rows_of(row), :]
+
+    def a_copy(step, flip):
+        ref = region(*block(step), flip)
+        return copy_to(peer, ref, ref, asend.at[flip, step], arecv.at[flip, step])
+
+    def cross_copy(step, whose):
+        ref = region(*block(step, whose), 0)
+        return copy_to(twin, ref, ref, csend.at[step], crecv.at[step])
+
+    def forward_copy(step, flip):
+        ref = region(*block(step, 1 - side), flip)
+        return copy_to(peer, ref, ref, fsend.at[flip, step], frecv.at[flip, step])
+
+    def both(row, col, act):
+        act(0)
+
+        @pl.when(row != col)
+        def _():
+            act(1)
+
+    def finish(step, slot):
+        row, col = block(step)
+        val = (own_ref[...] + got_ref[slot]).astype(BF16)
+        a_ref[row, rows_of(col), :] = val.T
+        a_ref[col, rows_of(row), :] = val
+
+    def finish_send(step):
+        @pl.when(step < SPLIT)
+        def _():
+            cross_copy(step, side).start()
+
+        row, col = block(step)
+        both(row, col, lambda flip: a_copy(step, flip).start())
+
+    def receive(step):
+        row, col = block(step, 1 - side)
+        cross_copy(step, 1 - side).wait_recv()
+
+        @pl.when(row != col)
+        def _():
+            a_ref[row, rows_of(col), :] = a_ref[col, rows_of(row), :].T
+
+        both(row, col, lambda flip: forward_copy(step, flip).start())
+
+    def product(step):
+        row, col = block(step)
+        return dot_tn(x_ref[row], x_ref[col])
+
+    def gram(k, _):
+        theirs = 2 * k + 1 - core
+        own = 2 * k + core
+        for late, first, last in ((0, 0, 3), (1, 3, 5), (2, 5, 6)):
+            @pl.when(k == late)
+            def _():
+                for pos in range(first, last):
+                    x_load(pos).wait()
+
+        @pl.when(k >= 1)
+        def _():
+            part_copy(theirs - 2).wait_send()
+            part_copy(own - 2).wait_recv()
+
+        before = jnp.maximum(k - 1, 0)
+        part_ref[...] = product(theirs)
+        finish(2 * before + core, jnp.where(k == 0, HALF, before))
+        part_copy(theirs).start()
+
+        @pl.when(k >= 1)
+        def _():
+            finish_send(own - 2)
+
+        for num in range(2):
+            @pl.when(k == 5 + num)
+            def _():
+                receive(2 * num + core)
+
+        own_ref[...] = product(own)
+        return 0
+
+    lax.fori_loop(0, HALF, gram, 0)
+    part_copy(STEPS - 1 - core).wait_send()
+    part_copy(STEPS - 2 + core).wait_recv()
+    finish(STEPS - 2 + core, HALF - 1)
+    finish_send(STEPS - 2 + core)
+
+    @pl.when(core == 0)
+    def _():
+        receive(SPLIT - 1)
+
+    def wait_got(k, _):
+        step = 2 * k + 1 - core
+        both(*block(step), lambda flip: a_copy(step, flip).wait_recv())
+        return 0
+
+    def wait_forward(k, _):
+        step = 2 * k + 1 - core
+        both(*block(step, 1 - side), lambda flip: forward_copy(step, flip).wait_recv())
+        return 0
+
+    lax.fori_loop(0, HALF, wait_got, 0)
+    lax.fori_loop(0, 2 + core, wait_forward, 0)
+
+    def b_copies(num, flip):
+        row, col = tri_index(num, NUM_BLK)
         if flip:
             row, col = col, row
-        ref = a_ref.at[col, rows_of(row), :]
-        return pltpu.make_async_remote_copy(
-            src_ref=ref, dst_ref=ref, send_sem=asend.at[flip, num], recv_sem=arecv.at[flip, num],
-            device_id=peer, device_id_type=MESH)
-
-    def finish(num):
-        row, col = tri_index(num, num_blk)
-        part_copy(num).wait_recv()
-        val = part_ref[num % 2] + got_ref[num // 2]
-        a_ref[col, rows_of(row), :] = val.astype(BF16)
-        a_copy(num, 0).start()
-
-        @pl.when(row != col)
-        def _():
-            a_ref[row, rows_of(col), :] = val.T.astype(BF16)
-            a_copy(num, 1).start()
-
-    def gram(step, _):
-        row, col = tri_index(step, num_blk)
-
-        @pl.when(row == 0)
-        def _():
-            x_load(col).wait()
-
-        part_ref[step % 2] = dot_tn(x_ref[row], x_ref[col])
-        mine = (step + core) % 2 == 0
-        theirs = (step + core) % 2 == 1
-
-        @pl.when(theirs)
-        def _():
-            part_copy(step).start()
-
-        @pl.when(jnp.logical_and(step >= 1, theirs))
-        def _():
-            finish(step - 1)
-
-        @pl.when(jnp.logical_and(step >= 1, mine))
-        def _():
-            part_copy(step - 1).wait_send()
-
-        return 0
-
-    lax.fori_loop(0, total, gram, 0)
-    last_mine = (total - 1 + core) % 2 == 0
-    last_theirs = (total - 1 + core) % 2 == 1
-
-    @pl.when(last_mine)
-    def _():
-        finish(total - 1)
-
-    @pl.when(last_theirs)
-    def _():
-        part_copy(total - 1).wait_send()
-
-    num_mine = (total + 1) // 2 - (total % 2) * core
-    num_theirs = total // 2 + (total % 2) * core
-
-    def wait_sent(k, _):
-        num = 2 * k + core
-        row, col = tri_index(num, num_blk)
-        a_copy(num, 0).wait_send()
-
-        @pl.when(row != col)
-        def _():
-            a_copy(num, 1).wait_send()
-
-        return 0
-
-    def wait_got(k, _):
-        num = 2 * k + 1 - core
-        row, col = tri_index(num, num_blk)
-        a_copy(num, 0).wait_recv()
-
-        @pl.when(row != col)
-        def _():
-            a_copy(num, 1).wait_recv()
-
-        return 0
-
-    lax.fori_loop(0, num_theirs, wait_got, 0)
-    lax.fori_loop(0, num_mine, wait_sent, 0)
-
-    def b_copies(num, flip):
-        slot = (num // 2) % 2
-        row, col = tri_index(num, num_blk)
-        if flip:
-            row, col = col, row
-        src = stage_ref.at[slot, flip]
+        src = stage_ref.at[(num // 2) % 2, flip]
         dst = b_ref.at[rows_of(row), rows_of(col)]
         local = pltpu.make_async_copy(src, dst, bloc.at[flip, num])
-        remote = pltpu.make_async_remote_copy(
-            src_ref=src, dst_ref=dst, send_sem=bsend.at[flip, num], recv_sem=brecv.at[flip, num],
-            device_id=peer, device_id_type=MESH)
-        return local, remote
+        return local, copy_to(peer, src, dst, bsend.at[flip, num], brecv.at[flip, num])
+
+    def b_start(num):
+        def act(flip):
+            local, remote = b_copies(num, flip)
+            remote.start()
+            local.start()
+
+        both(*tri_index(num, NUM_BLK), act)
 
     def b_drain(num):
-        row, col = tri_index(num, num_blk)
-        local, remote = b_copies(num, 0)
-        local.wait()
-        remote.wait_send()
-
-        @pl.when(row != col)
-        def _():
-            local, remote = b_copies(num, 1)
+        def act(flip):
+            local, remote = b_copies(num, flip)
             local.wait()
             remote.wait_send()
 
+        both(*tri_index(num, NUM_BLK), act)
+
+    def combine(num, slot):
+        row, col = tri_index(num, NUM_BLK)
+        gram_sq = sq_ref[...].astype(BF16)
+        val = a_ref[col, rows_of(row), :]
+        val = (COEF_B * val.astype(F32) + COEF_C * gram_sq.astype(F32)).astype(BF16)
+        stage_ref[slot, 0] = val
+        stage_ref[slot, 1] = val.T
+
+    num_mine = (total + 1) // 2 - core
+
     def square(k, _):
         num = 2 * k + core
-        row, col = tri_index(num, num_blk)
-        slot = k % 2
-
-        @pl.when(k >= 2)
-        def _():
-            b_drain(num - 4)
-
-        gram_sq = dot_tn(a_ref[row], a_ref[col]).astype(BF16)
-        gram = a_ref[col, rows_of(row), :]
-        poly = COEF_B * gram.astype(F32) + COEF_C * gram_sq.astype(F32)
-        stage_ref[slot, 0] = poly.astype(BF16)
-        local, remote = b_copies(num, 0)
-        remote.start()
-        local.start()
-
-        @pl.when(row != col)
-        def _():
-            stage_ref[slot, 1] = poly.T.astype(BF16)
-            local, remote = b_copies(num, 1)
-            remote.start()
-            local.start()
+
+        @pl.when(k >= 3)
+        def _():
+            b_drain(num - 6)
+
+        combine(2 * jnp.maximum(k - 1, 0) + core, (k + 1) % 2)
+        row, col = tri_index(num, NUM_BLK)
+        sq_ref[...] = dot_tn(a_ref[row], a_ref[col])
+
+        @pl.when(k >= 1)
+        def _():
+            b_start(num - 2)
 
         return 0
 
     lax.fori_loop(0, num_mine, square, 0)
-    b_drain(2 * (num_mine - 2) + core)
-    b_drain(2 * (num_mine - 1) + core)
+    last = 2 * (num_mine - 1) + core
+    b_drain(last - 4)
+    combine(last, (num_mine - 1) % 2)
+    b_start(last)
+
+    def wait_sent(k, _):
+        step = 2 * k + core
+        both(*block(step), lambda flip: a_copy(step, flip).wait_send())
+        return 0
+
+    def wait_crossed(k, _):
+        step = 2 * k + core
+        cross_copy(step, side).wait_send()
+        both(*block(step, 1 - side), lambda flip: forward_copy(step, flip).wait_send())
+        return 0
 
     def wait_b(k, _):
         num = 2 * k + 1 - core
-        row, col = tri_index(num, num_blk)
-        b_copies(num, 0)[1].wait_recv()
-
-        @pl.when(row != col)
-        def _():
-            b_copies(num, 1)[1].wait_recv()
-
-        return 0
-
-    lax.fori_loop(0, num_theirs, wait_b, 0)
+        both(*tri_index(num, NUM_BLK), lambda flip: b_copies(num, flip)[1].wait_recv())
+        return 0
+
+    lax.fori_loop(0, HALF, wait_sent, 0)
+    lax.fori_loop(0, 3 - core, wait_crossed, 0)
+    b_drain(last - 2)
+    b_drain(last)
+    lax.fori_loop(0, total - num_mine, wait_b, 0)
 
 
 def poly(x_mat):
     rows, cols = x_mat.shape
-    num_blk = cols // BLK
-    total = num_blk * (num_blk + 1) // 2
-    half = (total + 1) // 2
+    total = NUM_BLK * (NUM_BLK + 1) // 2
     dma = pltpu.SemaphoreType.DMA
     return pl.pallas_call(
-        functools.partial(poly_kernel, num_blk),
+        poly_kernel,
         out_shape=jax.ShapeDtypeStruct((cols, cols), BF16),
         in_specs=[pl.BlockSpec(memory_space=pl.ANY)],
         out_specs=pl.BlockSpec(memory_space=pl.ANY),
         scratch_shapes=[
-            pltpu.VMEM((num_blk, rows, BLK), BF16),
-            pltpu.VMEM((num_blk, cols, BLK), BF16),
-            pltpu.VMEM((2, BLK, BLK), F32),
-            pltpu.VMEM((half, BLK, BLK), F32),
+            pltpu.VMEM((NUM_BLK, rows, BLK), BF16),
+            pltpu.VMEM((NUM_BLK, cols, BLK), BF16),
+            pltpu.VMEM((BLK, BLK), F32),
+            pltpu.VMEM((BLK, BLK), F32),
+            pltpu.VMEM((BLK, BLK), F32),
+            pltpu.VMEM((HALF + 1, BLK, BLK), F32),
             pltpu.VMEM((2, 2, BLK, BLK), BF16),
-            dma((num_blk,)), dma((total,)), dma((total,)),
-            dma((2, total)), dma((2, total)),
+            dma((NUM_BLK,)), dma((STEPS,)), dma((STEPS,)),
+            dma((2, STEPS)), dma((2, STEPS)),
+            dma((SPLIT,)), dma((SPLIT,)),
+            dma((2, SPLIT)), dma((2, SPLIT)),
             dma((2, total)), dma((2, total)), dma((2, total)),
         ],
         compiler_params=pltpu.CompilerParams(

time: 1230 us -> 1180 us (0.959)
  Pallas kernels: 1150 us -> 1100 us
    pallas_call x5, Pallas kernels: 429 us -> 378 us  [poly(): pl.pallas_call(poly_kernel, out_shape=jax.ShapeDtypeStruct((cols, cols),...]
where the time goes in v3:
time: 1180 us; the launch traced here: 1170 us
  Pallas kernels  1100 us (93%)
  waiting for transfers between devices  43.4 us (4%)
  other arithmetic  22.7 us (2%)
    pallas_call x5, Pallas kernels, poly(): pl.pallas_call(poly_kernel, out_shape=jax.ShapeDtypeStruct((cols, cols),...  378 us
    pallas_call x4, Pallas kernels, update(): pl.pallas_call(functools.partial(update_kernel, col_tile), grid=(cols //...  344 us
    pallas_call x1, Pallas kernels, spread(): pl.pallas_call(functools.partial(spread_kernel, rows, cols), out_shape=ja...  281 us
    pallas_call x3, Pallas kernels, last_pieces(): pl.pallas_call(functools.partial(pair_kernel, tile, base), grid_spec=pltp...  61.4 us
    ppermute x5, waiting for transfers between devices, permute(): return lax.ppermute(piece, ('fsdp', 'tp'), pairs)  43.4 us
    pallas_call x6, Pallas kernels, apply_piece(): pl.pallas_call(apply_kernel, grid_spec=pltpu.PrefetchScalarGridSpec(num_s...  32.2 us
  transfers between devices with their start and end apart: 5, of which 2 were waited for; matrix products, arithmetic and copies ran while one was open for 0% of the time, Pallas kernels for 2%

profile of v3, /device:TPU:0, one launch (start us, length us, event | category | flops | bytes accessed | tf_op | source)
XLA Modules:
  0.0 1171.5 jit_solution(14310346159057048595)
XLA Ops:
  2.6 0.7 pad_maximum_fusion.scale_ref
  3.3 0.1 stack.103
  3.4 0.1 stack.98
  3.4 21.5 %fusion.1 = (f32[2]{0:T(128)S(1)}, f32[2,4096,768]{2,1,0:T(8,128)}) fusion(bf16[2,4096,768]{2,1,0:T(8,128)(2,1)} %g_ref.1, f32[]{:T(128)} %copy.19, f32[2,4096,768]{2,1,0:T(8,128)} %m_ref.1), kind=kLoop, calls=%fused_computation.3 | loop fusion | flops 44040192 | bytes 62914572 | tf_op jit(solution)/shard_map/reduce_sum | solution.py:559
  25.0 0.1 stack.93
  25.0 0.1 stack.109
  25.1 0.6 pad_add_fusion
  25.7 0.7 scatter.8.sq_ref
  26.3 281.2 %spread.1.x_hbm.x_ref = bf16[4096,3072]{1,0:T(8,128)(2,1)} custom-call(f32[1]{0:T(128)} %bitcast.20.mu_ref, f32[8,128]{1,0:T(8,128)} %scatter.8.sq_ref, f32[2,4096,768]{2,1,0:T(8,128)} %m_ref.1, bf16[2,4096,768]{2,1,0:T(8,128)(2,1)} %g_ref.1), custom_call_target="tpu_custom_call" | custom-call | tf_op jit(solution)/shard_map/spread/pallas_call | solution.py:176
  307.6 74.9 %poly.5.b_ref = bf16[3072,3072]{1,0:T(8,128)(2,1)} custom-call(bf16[4096,3072]{1,0:T(8,128)(2,1)} %spread.1.x_hbm.x_ref), custom_call_target="tpu_custom_call" | custom-call | tf_op jit(solution)/shard_map/poly/pallas_call | solution.py:428
  382.5 86.0 %update.4.x_hbm.x_ref = bf16[4096,3072]{1,0:T(8,128)(2,1)} custom-call(bf16[4096,3072]{1,0:T(8,128)(2,1)} %spread.1.x_hbm.x_ref, bf16[3072,3072]{1,0:T(8,128)(2,1)} %poly.5.b_ref), custom_call_target="tpu_custom_call" | custom-call | tf_op jit(solution)/shard_map/update/pallas_call | solution.py:462
  468.6 76.6 %poly.6.b_ref = bf16[3072,3072]{1,0:T(8,128)(2,1)} custom-call(bf16[4096,3072]{1,0:T(8,128)(2,1)} %update.4.x_hbm.x_ref), custom_call_target="tpu_custom_call" | custom-call | tf_op jit(solution)/shard_map/poly/pallas_call | solution.py:428
  545.2 86.2 %update.5.x_hbm.x_ref = bf16[4096,3072]{1,0:T(8,128)(2,1)} custom-call(bf16[4096,3072]{1,0:T(8,128)(2,1)} %update.4.x_hbm.x_ref, bf16[3072,3072]{1,0:T(8,128)(2,1)} %poly.6.b_ref), custom_call_target="tpu_custom_call" | custom-call | tf_op jit(solution)/shard_map/update/pallas_call | solution.py:462
  631.3 74.8 %poly.7.b_ref = bf16[3072,3072]{1,0:T(8,128)(2,1)} custom-call(bf16[4096,3072]{1,0:T(8,128)(2,1)} %update.5.x_hbm.x_ref), custom_call_target="tpu_custom_call" | custom-call | tf_op jit(solution)/shard_map/poly/pallas_call | solution.py:428
  706.2 86.0 %update.6.x_hbm.x_ref = bf16[4096,3072]{1,0:T(8,128)(2,1)} custom-call(bf16[4096,3072]{1,0:T(8,128)(2,1)} %update.5.x_hbm.x_ref, bf16[3072,3072]{1,0:T(8,128)(2,1)} %poly.7.b_ref), custom_call_target="tpu_custom_call" | custom-call | tf_op jit(solution)/shard_map/update/pallas_call | solution.py:462
  792.2 76.6 %poly.8.b_ref = bf16[3072,3072]{1,0:T(8,128)(2,1)} custom-call(bf16[4096,3072]{1,0:T(8,128)(2,1)} %update.6.x_hbm.x_ref), custom_call_target="tpu_custom_call" | custom-call | tf_op jit(solution)/shard_map/poly/pallas_call | solution.py:428
  868.8 86.2 %update.7.x_hbm.x_ref = bf16[4096,3072]{1,0:T(8,128)(2,1)} custom-call(bf16[4096,3072]{1,0:T(8,128)(2,1)} %update.6.x_hbm.x_ref, bf16[3072,3072]{1,0:T(8,128)(2,1)} %poly.8.b_ref), custom_call_target="tpu_custom_call" | custom-call | tf_op jit(solution)/shard_map/update/pallas_call | solution.py:462
  955.0 74.8 %poly.9.b_ref = bf16[3072,3072]{1,0:T(8,128)(2,1)} custom-call(bf16[4096,3072]{1,0:T(8,128)(2,1)} %update.7.x_hbm.x_ref), custom_call_target="tpu_custom_call" | custom-call | tf_op jit(solution)/shard_map/poly/pallas_call | solution.py:428
  1029.8 17.0 %last_pieces.3 = (bf16[1024,768]{1,0:T(8,128)(2,1)}, bf16[1024,768]{1,0:T(8,128)(2,1)}) custom-call(s32[2,6]{1,0:T(2,128)} %get-tuple-element.28.tab_ref, bf16[4096,3072]{1,0:T(8,128)(2,1)} %update.7.x_hbm.x_ref, bf16[3072,3072]{1,0:T(8,128)(2,1)} %poly.9.b_ref), custom_call_target="tpu_custom_call" | custom-call | flops 9663676416 | bytes 22020096 | tf_op jit(solution)/shard_map/last_pieces/pallas_call | solution.py:497
  1046.8 16.9 %last_pieces.4 = (bf16[1024,768]{1,0:T(8,128)(2,1)}, bf16[1024,768]{1,0:T(8,128)(2,1)}) custom-call(s32[2,6]{1,0:T(2,128)} %get-tuple-element.28.tab_ref, bf16[4096,3072]{1,0:T(8,128)(2,1)} %update.7.x_hbm.x_ref, bf16[3072,3072]{1,0:T(8,128)(2,1)} %poly.9.b_ref), custom_call_target="tpu_custom_call" | custom-call | flops 9663676416 | bytes 22020096 | tf_op jit(solution)/shard_map/last_pieces/pallas_call | solution.py:497
  1063.7 27.5 %last_pieces.5 = (bf16[2048,768]{1,0:T(8,128)(2,1)}, bf16[2048,768]{1,0:T(8,128)(2,1)}) custom-call(s32[2,6]{1,0:T(2,128)} %get-tuple-element.28.tab_ref, bf16[4096,3072]{1,0:T(8,128)(2,1)} %update.7.x_hbm.x_ref, bf16[3072,3072]{1,0:T(8,128)(2,1)} %poly.9.b_ref), custom_call_target="tpu_custom_call" | custom-call | flops 19327352832 | bytes 34603008 | tf_op jit(solution)/shard_map/last_pieces/pallas_call | solution.py:497
  1091.2 0.9 collective-permute-start.4
  1092.0 1.3 collective-permute-start.3
  1093.3 0.9 collective-permute-start.2
  1094.2 0.6 collective-permute-start.1
  1094.8 0.7 collective-permute-start
  1095.5 7.3 apply_piece.6.rest_0_
  1102.9 0.0 collective-permute-done.4.x_ref
  1102.9 7.4 apply_piece.7.rest_0_
  1110.2 19.4 %collective-permute-done.3.x_ref = bf16[1024,768]{1,0:T(8,128)(2,1)} collective-permute-done((bf16[1024,768]{1,0:T(8,128)(2,1)}, bf16[1024,768]{1,0:T(8,128)(2,1)}, u32[]{:S(2)}, u32[]{:S(2)}) %collective-permute-start.3) | collective-permute-done | bytes 1572896 | tf_op jit(solution)/shard_map/ppermute | solution.py:595
  1129.6 4.4 apply_piece.8.rest_0_
  1134.0 0.0 collective-permute-done.2.x_ref
  1134.0 4.4 apply_piece.9.rest_0_
  1138.4 24.0 %collective-permute-done.1.x_ref = bf16[1024,768]{1,0:T(8,128)(2,1)} collective-permute-done((bf16[1024,768]{1,0:T(8,128)(2,1)}, bf16[1024,768]{1,0:T(8,128)(2,1)}, u32[]{:S(2)}, u32[]{:S(2)}) %collective-permute-start.1) | collective-permute-done | bytes 1572896 | tf_op jit(solution)/shard_map/ppermute | solution.py:595
  1162.3 4.4 apply_piece.10.rest_0_
  1166.7 0.0 collective-permute-done.x_ref
  1166.7 4.4 apply_piece.11
  (1 shorter events, 0.0 us)
Async XLA Ops:
  1091.2 11.7 collective-permute-start.4
  1092.0 37.6 %collective-permute-start.3 = (bf16[1024,768]{1,0:T(8,128)(2,1)}, bf16[1024,768]{1,0:T(8,128)(2,1)}, u32[]{:S(2)}, u32[]{:S(2)}) collective-permute-start(bf16[1024,768]{1,0:T(8,128)(2,1)} %get-tuple-element.30), channel_id=1, source_target_pairs={{0,2},{1,3},{2,0},{3,1},{4,6},{5,7},{6,4},{7,5}} | collective-permute-start | bytes 4718600 | tf_op jit(solution)/shard_map/ppermute | solution.py:595
  1093.3 40.7 %collective-permute-start.2 = (bf16[1024,768]{1,0:T(8,128)(2,1)}, bf16[1024,768]{1,0:T(8,128)(2,1)}, u32[]{:S(2)}, u32[]{:S(2)}) collective-permute-start(bf16[1024,768]{1,0:T(8,128)(2,1)} %get-tuple-element.31), channel_id=1, source_target_pairs={{0,5},{1,4},{2,7},{3,6},{4,1},{5,0},{6,3},{7,2}} | collective-permute-start | bytes 4718600 | tf_op jit(solution)/shard_map/ppermute | solution.py:595
  1094.2 68.2 %collective-permute-start.1 = (bf16[1024,768]{1,0:T(8,128)(2,1)}, bf16[1024,768]{1,0:T(8,128)(2,1)}, u32[]{:S(2)}, u32[]{:S(2)}) collective-permute-start(bf16[1024,768]{1,0:T(8,128)(2,1)} %get-tuple-element.34), channel_id=1, source_target_pairs={{0,2},{1,3},{2,0},{3,1},{4,6},{5,7},{6,4},{7,5}} | collective-permute-start | bytes 4718600 | tf_op jit(solution)/shard_map/ppermute | solution.py:595
  1094.8 71.9 %collective-permute-start = (bf16[1024,768]{1,0:T(8,128)(2,1)}, bf16[1024,768]{1,0:T(8,128)(2,1)}, u32[]{:S(2)}, u32[]{:S(2)}) collective-permute-start(bf16[1024,768]{1,0:T(8,128)(2,1)} %get-tuple-element.33), channel_id=1, source_target_pairs={{0,5},{1,4},{2,7},{3,6},{4,1},{5,0},{6,3},{7,2}} | collective-permute-start | bytes 4718600 | tf_op jit(solution)/shard_map/ppermute | solution.py:595

commit v4 on v3

--- a/solution.py
+++ b/solution.py
@@ -210,7 +210,8 @@
     twin = {'fsdp': 1 - side, 'tp': 2 * (1 - chip) + core}
 
     def x_load(pos):
-        blk = pos + side * (4 * int(pos == 1) - int(pos > 1))
+        other = (1 - core, 5 * core, 5 - 4 * core, 2, 3, 4)[pos]
+        blk = pos * (1 - side) + other * side
         return pltpu.make_async_copy(
             x_hbm.at[:, pl.ds(pl.multiple_of(blk * BLK, BLK), BLK)], x_ref.at[blk], xsem.at[pos])
 
@@ -289,7 +290,7 @@
     def gram(k, _):
         theirs = 2 * k + 1 - core
         own = 2 * k + core
-        for late, first, last in ((0, 0, 3), (1, 3, 5), (2, 5, 6)):
+        for late, first, last in ((0, 0, 2), (1, 3, 5), (2, 5, 6)):
             @pl.when(k == late)
             def _():
                 for pos in range(first, last):
@@ -313,6 +314,10 @@
             @pl.when(k == 5 + num)
             def _():
                 receive(2 * num + core)
+
+        @pl.when(k == 0)
+        def _():
+            x_load(2).wait()
 
         own_ref[...] = product(own)
         return 0
@@ -490,7 +495,7 @@
         out1_ref[...] = val
 
 
-def last_pieces(x_mat, b_mat, table, base, piece_rows, row_tile=1024):
+def last_pieces(x_mat, b_mat, table, base, piece_rows, row_tile=512):
     _, cols = x_mat.shape
     tile = cols // 4
     last = piece_rows // row_tile - 1
@@ -561,8 +566,8 @@
         half = sub // 2
         mat = (fsdp + chip) % 2
         far = 1 - mat
-        r_here, r_far = fsdp * (sub // 1024), (1 - fsdp) * (sub // 1024)
-        step = half // 1024
+        r_here, r_far = fsdp * (sub // 512), (1 - fsdp) * (sub // 512)
+        step = half // 512
         x_col, y_col = 2 * (1 - chip) + core, 2 * chip + 1 - core
         piece_tab = jnp.stack([
             jnp.stack([r_here, r_far, r_here + step, r_far + step, r_here, r_here]),

time: 1180 us -> 1170 us (level)
  no operation moved by 1% of the time
where the time goes in v4:
time: 1170 us
  Pallas kernels  1090 us (93%)
  waiting for transfers between devices  43.6 us (4%)
  other arithmetic  22.7 us (2%)
    pallas_call x5, Pallas kernels, poly(): pl.pallas_call(poly_kernel, out_shape=jax.ShapeDtypeStruct((cols, cols),...  372 us
    pallas_call x4, Pallas kernels, update(): pl.pallas_call(functools.partial(update_kernel, col_tile), grid=(cols //...  344 us
    pallas_call x1, Pallas kernels, spread(): pl.pallas_call(functools.partial(spread_kernel, rows, cols), out_shape=ja...  281 us
    pallas_call x3, Pallas kernels, last_pieces(): pl.pallas_call(functools.partial(pair_kernel, tile, base), grid_spec=pltp...  61.7 us
    ppermute x5, waiting for transfers between devices, permute(): return lax.ppermute(piece, ('fsdp', 'tp'), pairs)  43.6 us
    pallas_call x6, Pallas kernels, apply_piece(): pl.pallas_call(apply_kernel, grid_spec=pltpu.PrefetchScalarGridSpec(num_s...  32.2 us
  transfers between devices with their start and end apart: 5, of which 2 were waited for; matrix products, arithmetic and copies ran while one was open for 0% of the time, Pallas kernels for 2%

profile of v4, /device:TPU:0, one launch (start us, length us, event | category | flops | bytes accessed | tf_op | source)
XLA Modules:
  0.0 1165.5 jit_solution(4191341496194018291)
XLA Ops:
  2.6 0.7 pad_maximum_fusion.scale_ref
  3.3 0.1 stack.103
  3.4 0.1 stack.98
  3.4 21.5 %fusion.1 = (f32[2]{0:T(128)S(1)}, f32[2,4096,768]{2,1,0:T(8,128)}) fusion(bf16[2,4096,768]{2,1,0:T(8,128)(2,1)} %g_ref.1, f32[]{:T(128)} %copy.19, f32[2,4096,768]{2,1,0:T(8,128)} %m_ref.1), kind=kLoop, calls=%fused_computation.3 | loop fusion | flops 44040192 | bytes 62914572 | tf_op jit(solution)/shard_map/reduce_sum | solution.py:564
  25.0 0.1 stack.93
  25.0 0.1 stack.109
  25.1 0.6 pad_add_fusion
  25.7 0.7 scatter.8.sq_ref
  26.3 281.2 %spread.1.x_hbm.x_ref = bf16[4096,3072]{1,0:T(8,128)(2,1)} custom-call(f32[1]{0:T(128)} %bitcast.20.mu_ref, f32[8,128]{1,0:T(8,128)} %scatter.8.sq_ref, f32[2,4096,768]{2,1,0:T(8,128)} %m_ref.1, bf16[2,4096,768]{2,1,0:T(8,128)(2,1)} %g_ref.1), custom_call_target="tpu_custom_call" | custom-call | tf_op jit(solution)/shard_map/spread/pallas_call | solution.py:176
  307.6 73.7 %poly.5.b_ref = bf16[3072,3072]{1,0:T(8,128)(2,1)} custom-call(bf16[4096,3072]{1,0:T(8,128)(2,1)} %spread.1.x_hbm.x_ref), custom_call_target="tpu_custom_call" | custom-call | tf_op jit(solution)/shard_map/poly/pallas_call | solution.py:433
  381.3 86.0 %update.4.x_hbm.x_ref = bf16[4096,3072]{1,0:T(8,128)(2,1)} custom-call(bf16[4096,3072]{1,0:T(8,128)(2,1)} %spread.1.x_hbm.x_ref, bf16[3072,3072]{1,0:T(8,128)(2,1)} %poly.5.b_ref), custom_call_target="tpu_custom_call" | custom-call | tf_op jit(solution)/shard_map/update/pallas_call | solution.py:467
  467.4 75.4 %poly.6.b_ref = bf16[3072,3072]{1,0:T(8,128)(2,1)} custom-call(bf16[4096,3072]{1,0:T(8,128)(2,1)} %update.4.x_hbm.x_ref), custom_call_target="tpu_custom_call" | custom-call | tf_op jit(solution)/shard_map/poly/pallas_call | solution.py:433
  542.7 86.2 %update.5.x_hbm.x_ref = bf16[4096,3072]{1,0:T(8,128)(2,1)} custom-call(bf16[4096,3072]{1,0:T(8,128)(2,1)} %update.4.x_hbm.x_ref, bf16[3072,3072]{1,0:T(8,128)(2,1)} %poly.6.b_ref), custom_call_target="tpu_custom_call" | custom-call | tf_op jit(solution)/shard_map/update/pallas_call | solution.py:467
  628.9 73.6 %poly.7.b_ref = bf16[3072,3072]{1,0:T(8,128)(2,1)} custom-call(bf16[4096,3072]{1,0:T(8,128)(2,1)} %update.5.x_hbm.x_ref), custom_call_target="tpu_custom_call" | custom-call | tf_op jit(solution)/shard_map/poly/pallas_call | solution.py:433
  702.5 86.0 %update.6.x_hbm.x_ref = bf16[4096,3072]{1,0:T(8,128)(2,1)} custom-call(bf16[4096,3072]{1,0:T(8,128)(2,1)} %update.5.x_hbm.x_ref, bf16[3072,3072]{1,0:T(8,128)(2,1)} %poly.7.b_ref), custom_call_target="tpu_custom_call" | custom-call | tf_op jit(solution)/shard_map/update/pallas_call | solution.py:467
  788.6 75.3 %poly.8.b_ref = bf16[3072,3072]{1,0:T(8,128)(2,1)} custom-call(bf16[4096,3072]{1,0:T(8,128)(2,1)} %update.6.x_hbm.x_ref), custom_call_target="tpu_custom_call" | custom-call | tf_op jit(solution)/shard_map/poly/pallas_call | solution.py:433
  863.9 86.2 %update.7.x_hbm.x_ref = bf16[4096,3072]{1,0:T(8,128)(2,1)} custom-call(bf16[4096,3072]{1,0:T(8,128)(2,1)} %update.6.x_hbm.x_ref, bf16[3072,3072]{1,0:T(8,128)(2,1)} %poly.8.b_ref), custom_call_target="tpu_custom_call" | custom-call | tf_op jit(solution)/shard_map/update/pallas_call | solution.py:467
  950.1 73.6 %poly.9.b_ref = bf16[3072,3072]{1,0:T(8,128)(2,1)} custom-call(bf16[4096,3072]{1,0:T(8,128)(2,1)} %update.7.x_hbm.x_ref), custom_call_target="tpu_custom_call" | custom-call | tf_op jit(solution)/shard_map/poly/pallas_call | solution.py:433
  1023.7 16.9 %last_pieces.3 = (bf16[1024,768]{1,0:T(8,128)(2,1)}, bf16[1024,768]{1,0:T(8,128)(2,1)}) custom-call(s32[2,6]{1,0:T(2,128)} %get-tuple-element.28.tab_ref, bf16[4096,3072]{1,0:T(8,128)(2,1)} %update.7.x_hbm.x_ref, bf16[3072,3072]{1,0:T(8,128)(2,1)} %poly.9.b_ref), custom_call_target="tpu_custom_call" | custom-call | flops 9663676416 | bytes 22020096 | tf_op jit(solution)/shard_map/last_pieces/pallas_call | solution.py:502
  1040.6 16.9 %last_pieces.4 = (bf16[1024,768]{1,0:T(8,128)(2,1)}, bf16[1024,768]{1,0:T(8,128)(2,1)}) custom-call(s32[2,6]{1,0:T(2,128)} %get-tuple-element.28.tab_ref, bf16[4096,3072]{1,0:T(8,128)(2,1)} %update.7.x_hbm.x_ref, bf16[3072,3072]{1,0:T(8,128)(2,1)} %poly.9.b_ref), custom_call_target="tpu_custom_call" | custom-call | flops 9663676416 | bytes 22020096 | tf_op jit(solution)/shard_map/last_pieces/pallas_call | solution.py:502
  1057.5 27.9 %last_pieces.5 = (bf16[2048,768]{1,0:T(8,128)(2,1)}, bf16[2048,768]{1,0:T(8,128)(2,1)}) custom-call(s32[2,6]{1,0:T(2,128)} %get-tuple-element.28.tab_ref, bf16[4096,3072]{1,0:T(8,128)(2,1)} %update.7.x_hbm.x_ref, bf16[3072,3072]{1,0:T(8,128)(2,1)} %poly.9.b_ref), custom_call_target="tpu_custom_call" | custom-call | flops 19327352832 | bytes 34603008 | tf_op jit(solution)/shard_map/last_pieces/pallas_call | solution.py:502
  1085.4 0.3 collective-permute-start.4
  1085.7 1.5 collective-permute-start.3
  1087.3 1.2 collective-permute-start.2
  1088.5 0.3 collective-permute-start.1
  1088.8 0.5 collective-permute-start
  1089.2 7.3 apply_piece.6.rest_0_
  1096.6 0.0 collective-permute-done.4.x_ref
  1096.6 7.4 apply_piece.7.rest_0_
  1103.9 19.4 %collective-permute-done.3.x_ref = bf16[1024,768]{1,0:T(8,128)(2,1)} collective-permute-done((bf16[1024,768]{1,0:T(8,128)(2,1)}, bf16[1024,768]{1,0:T(8,128)(2,1)}, u32[]{:S(2)}, u32[]{:S(2)}) %collective-permute-start.3) | collective-permute-done | bytes 1572896 | tf_op jit(solution)/shard_map/ppermute | solution.py:600
  1123.3 4.4 apply_piece.8.rest_0_
  1127.7 0.0 collective-permute-done.2.x_ref
  1127.7 4.4 apply_piece.9.rest_0_
  1132.1 24.2 %collective-permute-done.1.x_ref = bf16[1024,768]{1,0:T(8,128)(2,1)} collective-permute-done((bf16[1024,768]{1,0:T(8,128)(2,1)}, bf16[1024,768]{1,0:T(8,128)(2,1)}, u32[]{:S(2)}, u32[]{:S(2)}) %collective-permute-start.1) | collective-permute-done | bytes 1572896 | tf_op jit(solution)/shard_map/ppermute | solution.py:600
  1156.3 4.4 apply_piece.10.rest_0_
  1160.7 0.0 collective-permute-done.x_ref
  1160.7 4.4 apply_piece.11
  (1 shorter events, 0.0 us)
Async XLA Ops:
  1085.4 11.2 collective-permute-start.4
  1085.7 37.6 %collective-permute-start.3 = (bf16[1024,768]{1,0:T(8,128)(2,1)}, bf16[1024,768]{1,0:T(8,128)(2,1)}, u32[]{:S(2)}, u32[]{:S(2)}) collective-permute-start(bf16[1024,768]{1,0:T(8,128)(2,1)} %get-tuple-element.30), channel_id=1, source_target_pairs={{0,2},{1,3},{2,0},{3,1},{4,6},{5,7},{6,4},{7,5}} | collective-permute-start | bytes 4718600 | tf_op jit(solution)/shard_map/ppermute | solution.py:600
  1087.3 40.4 %collective-permute-start.2 = (bf16[1024,768]{1,0:T(8,128)(2,1)}, bf16[1024,768]{1,0:T(8,128)(2,1)}, u32[]{:S(2)}, u32[]{:S(2)}) collective-permute-start(bf16[1024,768]{1,0:T(8,128)(2,1)} %get-tuple-element.31), channel_id=1, source_target_pairs={{0,5},{1,4},{2,7},{3,6},{4,1},{5,0},{6,3},{7,2}} | collective-permute-start | bytes 4718600 | tf_op jit(solution)/shard_map/ppermute | solution.py:600
  1088.5 67.8 %collective-permute-start.1 = (bf16[1024,768]{1,0:T(8,128)(2,1)}, bf16[1024,768]{1,0:T(8,128)(2,1)}, u32[]{:S(2)}, u32[]{:S(2)}) collective-permute-start(bf16[1024,768]{1,0:T(8,128)(2,1)} %get-tuple-element.34), channel_id=1, source_target_pairs={{0,2},{1,3},{2,0},{3,1},{4,6},{5,7},{6,4},{7,5}} | collective-permute-start | bytes 4718600 | tf_op jit(solution)/shard_map/ppermute | solution.py:600
  1088.8 71.9 %collective-permute-start = (bf16[1024,768]{1,0:T(8,128)(2,1)}, bf16[1024,768]{1,0:T(8,128)(2,1)}, u32[]{:S(2)}, u32[]{:S(2)}) collective-permute-start(bf16[1024,768]{1,0:T(8,128)(2,1)} %get-tuple-element.33), channel_id=1, source_target_pairs={{0,5},{1,4},{2,7},{3,6},{4,1},{5,0},{6,3},{7,2}} | collective-permute-start | bytes 4718600 | tf_op jit(solution)/shard_map/ppermute | solution.py:600
